TPU v7x, 32 devices: a whole 2x2x4 slice. The times are simulated.
32 devices in a mesh: rows: 4 (over x, core), seq: 8 (over z, y).
Axes of the slice: x: 2, y: 2, z: 4, core: 2. Of those that a mesh axis runs over, the one named last changes fastest.
Arguments:
- layer_in: bfloat16 [32, 1024, 768], P('rows', 'seq'), may hold values from -6 to 6
- cotangent: bfloat16 [32, 1024, 768], P('rows', 'seq'), may hold values from -6 to 6
- seg_lengths: int32 [32, 4], P('rows'), may hold values from 1 to 384, as said below
- query_weight: bfloat16 [768, 768], P(('rows', 'seq')), may hold values from -0.21875 to 0.21875
- query_bias: bfloat16 [768], P(('rows', 'seq')), may hold values from -3 to 3
- key_weight: bfloat16 [768, 768], P(('rows', 'seq')), may hold values from -0.21875 to 0.21875
- value_weight: bfloat16 [768, 768], P(('rows', 'seq')), may hold values from -0.21875 to 0.21875
- value_bias: bfloat16 [768], P(('rows', 'seq')), may hold values from -3 to 3
- out_weight: bfloat16 [768, 768], P(('rows', 'seq')), may hold values from -0.875 to 0.875
- out_bias: bfloat16 [768], P(('rows', 'seq')), may hold values from -2 to 2
- attn_gain: bfloat16 [768], P(('rows', 'seq')), may hold values from 0.5 to 1.5
- attn_shift: bfloat16 [768], P(('rows', 'seq')), may hold values from -2 to 2
- inner_weight: bfloat16 [768, 3072], P(('rows', 'seq')), may hold values from -0.21875 to 0.21875
- inner_bias: bfloat16 [3072], P(('rows', 'seq')), may hold values from -3 to 3
- outer_weight: bfloat16 [3072, 768], P(('rows', 'seq')), may hold values from -0.21875 to 0.21875
- outer_bias: bfloat16 [768], P(('rows', 'seq')), may hold values from -2 to 2
- final_gain: bfloat16 [768], P(('rows', 'seq')), may hold values from 0.5 to 1.5
- final_shift: bfloat16 [768], P(('rows', 'seq')), may hold values from -2 to 2
Outputs:
- layer_out: bfloat16 [32, 1024, 768], P('rows', 'seq')
- grad_in: float32 [32, 1024, 768], P('rows', 'seq')
- grad_query_weight: float32 [768, 768], P(('rows', 'seq'))
- grad_query_bias: float32 [768], P(('rows', 'seq'))
- grad_key_weight: float32 [768, 768], P(('rows', 'seq'))
- grad_value_weight: float32 [768, 768], P(('rows', 'seq'))
- grad_value_bias: float32 [768], P(('rows', 'seq'))
- grad_out_weight: float32 [768, 768], P(('rows', 'seq'))
- grad_out_bias: float32 [768], P(('rows', 'seq'))
- grad_attn_gain: float32 [768], P(('rows', 'seq'))
- grad_attn_shift: float32 [768], P(('rows', 'seq'))
- grad_inner_weight: float32 [768, 3072], P(('rows', 'seq'))
- grad_inner_bias: float32 [3072], P(('rows', 'seq'))
- grad_outer_weight: float32 [3072, 768], P(('rows', 'seq'))
- grad_outer_bias: float32 [768], P(('rows', 'seq'))
- grad_final_gain: float32 [768], P(('rows', 'seq'))
- grad_final_shift: float32 [768], P(('rows', 'seq'))
Inputs may be any that keep to these rules, and one draw needn't show every extreme that they name: `seg_lengths`: the lengths of each row sum to 960, and the positions past their sum are padding; the last segment of each row has exactly 384 tokens.
All inputs are finite; a program needn't handle non-finite values.
Results may differ from a plain program's by a relative error of at most 0.015.
Values may be sent and summed in bfloat16 or wider, within the bound.
A program may use at most 256 MiB of HBM per device.

v0:
```python
from functools import partial

import jax
import jax.numpy as jnp
from jax import lax
from jax.sharding import PartitionSpec as P

HEADS = 12
HEAD_DIM = 64
REACH = 3


epsilon = 1e-12
masked_score = -1e30


def passed_along(block, axis, distance):
    devices = range(lax.axis_size(axis))
    route = [(i - distance, i) for i in devices if i - distance in devices]
    return lax.ppermute(block, axis, route)


def segment_ids(lengths, positions, row_len):
    seg_ends = jnp.cumsum(lengths, axis=1)
    seg_count = jnp.sum(
        (positions[None, None, :] >= seg_ends[:, :, None]).astype(jnp.int32), axis=1
    )
    real_token = positions[None, :] < seg_ends[:, -1:]
    inside = (positions >= 0) & (positions < row_len)
    seg_id = jnp.where(real_token, seg_count, row_len + positions[None, :])
    return jnp.where(inside[None, :], seg_id, -1)


def norm_parts(values):
    row_mean = jnp.mean(values, axis=-1, keepdims=True)
    centred = values - row_mean
    inv_std = lax.rsqrt(jnp.mean(centred * centred, axis=-1, keepdims=True) + epsilon)
    return (centred * inv_std, inv_std)


def norm_back(upstream, normed, inv_std, gain_vec):
    scaled = upstream * gain_vec
    return inv_std * (
        scaled
        - jnp.mean(scaled, axis=-1, keepdims=True)
        - normed * jnp.mean(scaled * normed, axis=-1, keepdims=True)
    )


def split_window(window, features):
    key_rows = window[:, :features].reshape(window.shape[0], HEADS, HEAD_DIM)
    value_rows = window[:, features:].reshape(window.shape[0], HEADS, HEAD_DIM)
    return (key_rows, value_rows)


def row_scores(query_rows, key_rows, same_segment, score_scale):
    scores = (
        jnp.einsum("qhd,khd->hqk", query_rows, key_rows, preferred_element_type=jnp.float32)
        * score_scale
    )
    return jnp.where(same_segment[None], scores, masked_score)


def attend_row(pieces, score_scale):
    query_rows, window, same_segment = pieces
    key_rows, value_rows = split_window(window, query_rows.shape[1] * query_rows.shape[2])
    scores = row_scores(query_rows, key_rows, same_segment, score_scale)
    row_max = jnp.max(scores, axis=-1, keepdims=True)
    weights = jnp.exp(scores - row_max)
    row_total = jnp.sum(weights, axis=-1, keepdims=True)
    weights_b = (weights / row_total).astype(jnp.bfloat16)
    context = jnp.einsum("hqk,khd->qhd", weights_b, value_rows, preferred_element_type=jnp.float32)
    return (context.astype(jnp.bfloat16), (row_max + jnp.log(row_total))[..., 0])


def attend_back(pieces, score_scale):
    query_rows, window, same_segment, logsum, grad_context = pieces
    features = query_rows.shape[1] * query_rows.shape[2]
    key_rows, value_rows = split_window(window, features)
    scores = row_scores(query_rows, key_rows, same_segment, score_scale)
    probs = jnp.exp(scores - logsum[..., None])
    grad_probs = jnp.einsum(
        "qhd,khd->hqk", grad_context, value_rows, preferred_element_type=jnp.float32
    )
    grad_scores = (
        probs * (grad_probs - jnp.sum(grad_probs * probs, axis=-1, keepdims=True))
    ).astype(jnp.bfloat16)
    grad_query = (
        jnp.einsum("hqk,khd->qhd", grad_scores, key_rows, preferred_element_type=jnp.float32)
        * score_scale
    )
    grad_key = (
        jnp.einsum("hqk,qhd->khd", grad_scores, query_rows, preferred_element_type=jnp.float32)
        * score_scale
    )
    grad_value = jnp.einsum(
        "hqk,qhd->khd", probs.astype(jnp.bfloat16), grad_context, preferred_element_type=jnp.float32
    )
    width_keys = window.shape[0]
    return (
        grad_query,
        jnp.concatenate(
            [grad_key.reshape(width_keys, features), grad_value.reshape(width_keys, features)],
            axis=1,
        ),
    )


def near_distances():
    return list(range(REACH, 0, -1)) + list(range(-1, -REACH - 1, -1))


def near_window(kv_local):
    lower_side = []
    upper_side = []
    for distance in near_distances():
        arrived = passed_along(kv_local, "seq", distance)
        if distance > 0:
            lower_side.append(arrived)
        else:
            upper_side.append(arrived)
    return jnp.concatenate(lower_side + [kv_local] + upper_side, axis=1)


def near_back(grad_window, block_len):
    own_grad = grad_window[:, REACH * block_len : (REACH + 1) * block_len]
    for position in range(2 * REACH + 1):
        offset = position - REACH
        if offset != 0:
            grad_piece = grad_window[:, position * block_len : (position + 1) * block_len]
            own_grad = own_grad + passed_along(
                grad_piece.astype(jnp.bfloat16), "seq", offset
            ).astype(grad_piece.dtype)
    return own_grad


def body(
    layer_in,
    cotangent,
    seg_lengths,
    query_weight,
    query_bias,
    key_weight,
    value_weight,
    value_bias,
    out_weight,
    out_bias,
    attn_gain,
    attn_shift,
    inner_weight,
    inner_bias,
    outer_weight,
    outer_bias,
    final_gain,
    final_shift,
):
    shards = (
        query_weight,
        query_bias,
        key_weight,
        value_weight,
        value_bias,
        out_weight,
        out_bias,
        attn_gain,
        attn_shift,
        inner_weight,
        inner_bias,
        outer_weight,
        outer_bias,
        final_gain,
        final_shift,
    )
    gathered = (
        lax.all_gather(shards[0], ("rows", "seq"), axis=0, tiled=True),
        lax.all_gather(shards[1], ("rows", "seq"), axis=0, tiled=True),
        lax.all_gather(shards[2], ("rows", "seq"), axis=0, tiled=True),
        lax.all_gather(shards[3], ("rows", "seq"), axis=0, tiled=True),
        lax.all_gather(shards[4], ("rows", "seq"), axis=0, tiled=True),
        lax.all_gather(shards[5], ("rows", "seq"), axis=0, tiled=True),
        lax.all_gather(shards[6], ("rows", "seq"), axis=0, tiled=True),
        lax.all_gather(shards[7], ("rows", "seq"), axis=0, tiled=True),
        lax.all_gather(shards[8], ("rows", "seq"), axis=0, tiled=True),
        lax.all_gather(shards[9], ("rows", "seq"), axis=0, tiled=True),
        lax.all_gather(shards[10], ("rows", "seq"), axis=0, tiled=True),
        lax.all_gather(shards[11], ("rows", "seq"), axis=0, tiled=True),
        lax.all_gather(shards[12], ("rows", "seq"), axis=0, tiled=True),
        lax.all_gather(shards[13], ("rows", "seq"), axis=0, tiled=True),
        lax.all_gather(shards[14], ("rows", "seq"), axis=0, tiled=True),
    )
    (
        query_mat,
        query_vec,
        key_mat,
        value_mat,
        value_vec,
        out_mat,
        out_vec,
        attn_gain_f,
        attn_shift_f,
        inner_mat,
        inner_vec,
        outer_mat,
        outer_vec,
        final_gain_f,
        final_shift_f,
    ) = gathered
    row_count, block_len, features = layer_in.shape
    tokens = row_count * block_len
    score_scale = HEAD_DIM ** (-0.5)
    inputs = layer_in.reshape(tokens, features)
    query_flat = jnp.dot(inputs, query_mat, preferred_element_type=jnp.float32) + query_vec.astype(
        jnp.float32
    )
    query_b = query_flat.astype(jnp.bfloat16).reshape(row_count, block_len, HEADS, HEAD_DIM)
    kv_mat = jnp.concatenate([key_mat, value_mat], axis=1)
    kv_bias = jnp.concatenate([jnp.zeros_like(value_vec), value_vec]).astype(jnp.float32)
    kv_local = (
        (jnp.dot(inputs, kv_mat, preferred_element_type=jnp.float32) + kv_bias)
        .astype(jnp.bfloat16)
        .reshape(row_count, block_len, 2 * features)
    )
    seq_index = lax.axis_index("seq")
    row_len = block_len * lax.axis_size("seq")
    local_pos = seq_index * block_len + jnp.arange(block_len, dtype=jnp.int32)
    window_pos = (seq_index - REACH) * block_len + jnp.arange(
        (2 * REACH + 1) * block_len, dtype=jnp.int32
    )
    query_ids = segment_ids(seg_lengths, local_pos, row_len)
    key_ids = segment_ids(seg_lengths, window_pos, row_len)
    same_segment = query_ids[:, :, None] == key_ids[:, None, :]
    window = near_window(kv_local)
    context, logsum = lax.map(
        partial(attend_row, score_scale=score_scale), (query_b, window, same_segment)
    )
    context_flat = context.reshape(tokens, features)
    attended = jnp.dot(context_flat, out_mat, preferred_element_type=jnp.float32) + out_vec.astype(
        jnp.float32
    )
    first_sum = inputs.astype(jnp.float32) + attended
    normed_one, inv_std_one = norm_parts(first_sum)
    hidden = normed_one * attn_gain_f.astype(jnp.float32) + attn_shift_f.astype(jnp.float32)
    hidden_b = hidden.astype(jnp.bfloat16)
    inner_pre = jnp.dot(hidden_b, inner_mat, preferred_element_type=jnp.float32) + inner_vec.astype(
        jnp.float32
    )
    active, gelu_back = jax.vjp(partial(jax.nn.gelu, approximate=False), inner_pre)
    active_b = active.astype(jnp.bfloat16)
    outer_out = jnp.dot(active_b, outer_mat, preferred_element_type=jnp.float32) + outer_vec.astype(
        jnp.float32
    )
    normed_two, inv_std_two = norm_parts(hidden + outer_out)
    layer_out = (
        normed_two * final_gain_f.astype(jnp.float32) + final_shift_f.astype(jnp.float32)
    ).astype(jnp.bfloat16)
    real_token = (local_pos[None, :] < jnp.sum(seg_lengths, axis=1)[:, None]).astype(jnp.float32)
    upstream = (cotangent.astype(jnp.float32) * real_token[:, :, None]).reshape(tokens, features)
    grad_final_gain = jnp.sum(upstream * normed_two, axis=0)
    grad_final_shift = jnp.sum(upstream, axis=0)
    grad_second = norm_back(upstream, normed_two, inv_std_two, final_gain_f.astype(jnp.float32))
    grad_outer = grad_second.astype(jnp.bfloat16)
    grad_outer_bias = jnp.sum(grad_outer.astype(jnp.float32), axis=0)
    grad_outer_weight = jnp.einsum(
        "tf,td->fd", active_b, grad_outer, preferred_element_type=jnp.float32
    )
    grad_active = jnp.einsum("td,fd->tf", grad_outer, outer_mat, preferred_element_type=jnp.float32)
    grad_inner = gelu_back(grad_active)[0].astype(jnp.bfloat16)
    grad_inner_bias = jnp.sum(grad_inner.astype(jnp.float32), axis=0)
    grad_inner_weight = jnp.einsum(
        "td,tf->df", hidden_b, grad_inner, preferred_element_type=jnp.float32
    )
    grad_hidden = grad_second + jnp.einsum(
        "tf,df->td", grad_inner, inner_mat, preferred_element_type=jnp.float32
    )
    grad_attn_gain = jnp.sum(grad_hidden * normed_one, axis=0)
    grad_attn_shift = jnp.sum(grad_hidden, axis=0)
    grad_first = norm_back(grad_hidden, normed_one, inv_std_one, attn_gain_f.astype(jnp.float32))
    grad_attended = grad_first.astype(jnp.bfloat16)
    grad_out_bias = jnp.sum(grad_attended.astype(jnp.float32), axis=0)
    grad_out_weight = jnp.einsum(
        "td,te->de", context_flat, grad_attended, preferred_element_type=jnp.float32
    )
    grad_context = jnp.einsum(
        "te,de->td", grad_attended, out_mat, preferred_element_type=jnp.float32
    ).astype(jnp.bfloat16)
    grad_context = grad_context.reshape(row_count, block_len, HEADS, HEAD_DIM)
    grad_query, grad_window = lax.map(
        partial(attend_back, score_scale=score_scale),
        (query_b, window, same_segment, logsum, grad_context),
    )
    grad_kv = near_back(grad_window, block_len)
    grad_query_b = grad_query.reshape(tokens, features).astype(jnp.bfloat16)
    grad_kv_b = grad_kv.reshape(tokens, 2 * features).astype(jnp.bfloat16)
    grad_query_weight = jnp.einsum(
        "td,te->de", inputs, grad_query_b, preferred_element_type=jnp.float32
    )
    grad_query_bias = jnp.sum(grad_query_b.astype(jnp.float32), axis=0)
    grad_kv_weight = jnp.einsum("td,te->de", inputs, grad_kv_b, preferred_element_type=jnp.float32)
    grad_value_bias = jnp.sum(grad_kv_b[:, features:].astype(jnp.float32), axis=0)
    grad_in = grad_first + jnp.einsum(
        "te,de->td", grad_query_b, query_mat, preferred_element_type=jnp.float32
    )
    grad_in = grad_in + jnp.einsum(
        "te,de->td", grad_kv_b, kv_mat, preferred_element_type=jnp.float32
    )
    partial_grads = (
        grad_query_weight,
        grad_query_bias,
        grad_kv_weight[:, :features],
        grad_kv_weight[:, features:],
        grad_value_bias,
        grad_out_weight,
        grad_out_bias,
        grad_attn_gain,
        grad_attn_shift,
        grad_inner_weight,
        grad_inner_bias,
        grad_outer_weight,
        grad_outer_bias,
        grad_final_gain,
        grad_final_shift,
    )
    owned = (
        lax.psum_scatter(partial_grads[0], ("rows", "seq"), scatter_dimension=0, tiled=True),
        lax.psum_scatter(partial_grads[1], ("rows", "seq"), scatter_dimension=0, tiled=True),
        lax.psum_scatter(partial_grads[2], ("rows", "seq"), scatter_dimension=0, tiled=True),
        lax.psum_scatter(partial_grads[3], ("rows", "seq"), scatter_dimension=0, tiled=True),
        lax.psum_scatter(partial_grads[4], ("rows", "seq"), scatter_dimension=0, tiled=True),
        lax.psum_scatter(partial_grads[5], ("rows", "seq"), scatter_dimension=0, tiled=True),
        lax.psum_scatter(partial_grads[6], ("rows", "seq"), scatter_dimension=0, tiled=True),
        lax.psum_scatter(partial_grads[7], ("rows", "seq"), scatter_dimension=0, tiled=True),
        lax.psum_scatter(partial_grads[8], ("rows", "seq"), scatter_dimension=0, tiled=True),
        lax.psum_scatter(partial_grads[9], ("rows", "seq"), scatter_dimension=0, tiled=True),
        lax.psum_scatter(partial_grads[10], ("rows", "seq"), scatter_dimension=0, tiled=True),
        lax.psum_scatter(partial_grads[11], ("rows", "seq"), scatter_dimension=0, tiled=True),
        lax.psum_scatter(partial_grads[12], ("rows", "seq"), scatter_dimension=0, tiled=True),
        lax.psum_scatter(partial_grads[13], ("rows", "seq"), scatter_dimension=0, tiled=True),
        lax.psum_scatter(partial_grads[14], ("rows", "seq"), scatter_dimension=0, tiled=True),
    )
    g_qw, g_qb, g_kw, g_vw, g_vb, g_ow, g_ob, g_ag, g_as, g_iw, g_ib, g_tw, g_tb, g_fg, g_fs = owned
    return (
        layer_out.reshape(row_count, block_len, features),
        grad_in.reshape(row_count, block_len, features),
        g_qw,
        g_qb,
        g_kw,
        g_vw,
        g_vb,
        g_ow,
        g_ob,
        g_ag,
        g_as,
        g_iw,
        g_ib,
        g_tw,
        g_tb,
        g_fg,
        g_fs,
    )


def solution(mesh):
    placed = (
        P("rows", "seq", None),
        P("rows", "seq", None),
        P("rows", None),
        P(("rows", "seq"), None),
        P(("rows", "seq")),
        P(("rows", "seq"), None),
        P(("rows", "seq"), None),
        P(("rows", "seq")),
        P(("rows", "seq"), None),
        P(("rows", "seq")),
        P(("rows", "seq")),
        P(("rows", "seq")),
        P(("rows", "seq"), None),
        P(("rows", "seq")),
        P(("rows", "seq"), None),
        P(("rows", "seq")),
        P(("rows", "seq")),
        P(("rows", "seq")),
    )
    return jax.shard_map(
        body,
        mesh=mesh,
        in_specs=placed,
        out_specs=(
            P("rows", "seq", None),
            P("rows", "seq", None),
            P(("rows", "seq"), None),
            P(("rows", "seq")),
            P(("rows", "seq"), None),
            P(("rows", "seq"), None),
            P(("rows", "seq")),
            P(("rows", "seq"), None),
            P(("rows", "seq")),
            P(("rows", "seq")),
            P(("rows", "seq")),
            P(("rows", "seq"), None),
            P(("rows", "seq")),
            P(("rows", "seq"), None),
            P(("rows", "seq")),
            P(("rows", "seq")),
            P(("rows", "seq")),
        ),
        check_vma=False,
    )
```

profile of v0, /device:TPU:0, one launch (start us, length us, event | category | flops | bytes accessed | tf_op | source)
XLA Modules:
  0.0 1829.8 jit_solution(7902769398490669864)
XLA Ops:
  18.2 42.3 %all-reduce.20 = (bf16[768]{0:T(1024)(128)(2,1)S(1)}, bf16[768]{0:T(1024)(128)(2,1)S(1)}, bf16[768]{0:T(1024)(128)(2,1)S(1)}, bf16[768]{0:T(1024)(128)(2,1)S(1)}...) all-reduce(bf16[768]{0:T(1024)(128)(2,1)S(1)} %dynamic-update-slice, ...), channel_id=1, replica_groups=mesh['rows'=4,'seq'=8] {'rows','seq'}, use_global_device_ids=true, to_apply=%add.3 | all-reduce | flops 9216 | bytes 36864
  60.5 7.4 all-gather.7.cloned.1.call-done
  69.2 54.8 %all-gather.9.cloned.1.call-done = bf16[768,768]{1,0:T(8,128)(2,1)} async-done(((bf16[24,768]{1,0:T(8,128)(2,1)}), bf16[768,768]{1,0:T(8,128)(2,1)}) %all-gather.9.cloned.1.call-update) | async-done | bytes 1179664 | tf_op jit(solution)/shard_map/all_gather | solution.py:178
  126.8 4.7 add_convert_fusion.2
  131.6 2.8 copy.94
  134.4 3.6 collective-permute-start
  138.1 4.6 collective-permute-start.1
  142.7 5.0 collective-permute-start.2
  148.0 4.3 fusion.55
  155.5 104.2 %collective-permute-done = bf16[8,128,1536]{1,2,0:T(8,128)(2,1)S(1)} collective-permute-done((bf16[8,128,1536]{1,2,0:T(8,128)(2,1)}, bf16[8,128,1536]{1,2,0:T(8,128)(2,1)S(1)}, u32[]{:S(2)}, u32[]{:S(2)}) %collective-permute-start) | collective-permute-done | bytes 3145760 | tf_op jit(solution)/shard_map/ppermute | solution.py:20
  263.5 147.9 %all-gather.11.cloned.1.call-done = bf16[768,768]{1,0:T(8,128)(2,1)} async-done(((bf16[24,768]{1,0:T(8,128)(2,1)}), bf16[768,768]{1,0:T(8,128)(2,1)}) %all-gather.11.cloned.1.call-update) | async-done | bytes 1179664 | tf_op jit(solution)/shard_map/all_gather | solution.py:175
  411.4 4.3 add_convert_fusion.4
  435.9 7.3 copy-done
  443.2 64.7 %while.24 = (s32[]{:T(128)}, bf16[8,128,12,64]{1,3,2,0:T(8,128)(2,1)}, f32[8,12,128]{2,1,0:T(8,128)}, bf16[8,896,1536]{1,2,0:T(8,128)(2,1)}, pred[8,128,896]{2,1...) while((s32[]{:T(128)}, bf16[8,128,12,64]{1,3,2,0:T(8,128)(2,1)}, ...), condition=%wide.region_6.7_spmd, body=%wide.region_3.6_spmd.sunk | while | flops 368933376 | bytes 31295592 | solution.py:233
  507.9 4.7 copy.103
  514.5 3.9 fusion.74
  518.9 60.8 %all-gather.15.cloned.1.call-done = bf16[768,3072]{1,0:T(8,128)(2,1)} async-done(((bf16[24,3072]{1,0:T(8,128)(2,1)}), bf16[768,3072]{1,0:T(8,128)(2,1)}) %all-gather.15.cloned.1.call-update) | async-done | bytes 4718608 | tf_op jit(solution)/shard_map/all_gather | solution.py:184
  579.7 35.8 %multiply_convert_fusion.1 = (bf16[1024,3072]{1,0:T(8,128)(2,1)}, f32[1024,3072]{1,0:T(8,128)}, f32[1024,3072]{1,0:T(8,128)}) fusion(f32[3072]{0:T(1024)S(1)} %convert_element_type.160, bf16[768,3072]{1,0:T(8,128)(2,1)} %all-gather.15.cloned.1.call-done, f32[1024,768]{1,0:T(8,128)S(1)} %get-tuple-element.300, f32[768]{0:T(1024)S(1)} %convert_element_type.158, ...), kind=kOutput, calls=%fused_computation.56 | convolution fusion | flops 5043388416 | bytes 39348224 | tf_op jit(solution)/shard_map/dot_general | solution.py:244
  615.5 28.8 %all-gather.17.cloned.1.call-done = bf16[3072,768]{1,0:T(8,128)(2,1)} async-done(((bf16[96,768]{1,0:T(8,128)(2,1)}), bf16[3072,768]{1,0:T(8,128)(2,1)}) %all-gather.17.cloned.1.call-update) | async-done | bytes 4718608 | tf_op jit(solution)/shard_map/all_gather | solution.py:186
  644.3 8.8 fusion.75
  656.7 3.7 convert_reduce_fusion.1
  660.4 19.5 %convert_reduce_fusion = (f32[3072]{0:T(1024)}, bf16[1024,3072]{1,0:T(8,128)(2,1)}) fusion(f32[1024,3072]{1,0:T(8,128)} %get-tuple-element.280, bf16[3072,768]{1,0:T(8,128)(2,1)} %all-gather.17.cloned.1.call-done, f32[1024,768]{1,0:T(8,128)} %get-tuple-element.276, f32[1024,3072]{1,0:T(8,128)} %get-tuple-element.301, f32[3072]{0:T(1024)S(1)} %convert_element_type.160), kind=kOutput, calls=%fused_computation.54 | convolution fusion | flops 4886098944 | bytes 39346176 | tf_op jit(solution)/shard_map/td,fd->tf/dot_general | solution.py:266
  679.9 10.6 multiply_reduce_fusion.1
  697.6 225.8 %while.25 = (s32[]{:T(128)}, bf16[8,128,12,64]{1,3,2,0:T(8,128)(2,1)S(1)}, f32[8,896,1536]{2,1,0:T(8,128)}, bf16[8,896,1536]{1,2,0:T(8,128)(2,1)}, pred[8,128,89...) while((s32[]{:T(128)}, ...), condition=%wide.region_18.19_spmd, body=%wide.region_16.18_spmd.sunk | while | flops 903608832 | bytes 96761984 | solution.py:287
  714.7 6.1 copy.163
  720.8 5.3 constant_dynamic-update-slice_fusion.11
  742.8 6.1 copy.163
  749.0 5.4 constant_dynamic-update-slice_fusion.11
  768.3 2.7 maximum_bitcast_fusion.2
  771.0 6.1 copy.163
  777.2 5.3 constant_dynamic-update-slice_fusion.11
  799.1 6.1 copy.163
  805.3 5.3 constant_dynamic-update-slice_fusion.11
  827.3 6.1 copy.163
  833.4 5.4 constant_dynamic-update-slice_fusion.11
  855.5 6.1 copy.163
  861.7 5.3 constant_dynamic-update-slice_fusion.11
  883.6 6.1 copy.163
  889.8 5.4 constant_dynamic-update-slice_fusion.11
  911.9 6.1 copy.163
  918.0 5.3 constant_dynamic-update-slice_fusion.11
  923.3 23.9 %convert.8 = bf16[8,896,1536]{2,1,0:T(8,128)(2,1)} convert(f32[8,896,1536]{2,1,0:T(8,128)} %get-tuple-element.96) | non-fusion elementwise | flops 11010048 | bytes 66060288 | tf_op jit(solution)/shard_map/convert.5
  947.3 13.6 fusion.72
  962.2 2.8 fusion.48
  965.0 7.1 collective-permute-start.11
  972.1 6.7 collective-permute-start.10
  978.7 4.4 collective-permute-start.9
  984.4 51.9 %collective-permute-done.6 = bf16[8,128,1536]{2,1,0:T(8,128)(2,1)} collective-permute-done((bf16[8,128,1536]{2,1,0:T(8,128)(2,1)}, bf16[8,128,1536]{2,1,0:T(8,128)(2,1)}, u32[]{:S(2)}, u32[]{:S(2)}) %collective-permute-start.6) | collective-permute-done | bytes 3145760 | tf_op jit(solution)/shard_map/ppermute | solution.py:20
  1040.2 2.8 convolution_bitcast_fusion.1
  1045.1 57.5 %collective-permute-done.11 = bf16[8,128,1536]{2,1,0:T(8,128)(2,1)} collective-permute-done((bf16[8,128,1536]{2,1,0:T(8,128)(2,1)}, bf16[8,128,1536]{2,1,0:T(8,128)(2,1)}, u32[]{:S(2)}, u32[]{:S(2)}) %collective-permute-start.11) | collective-permute-done | bytes 3145760 | tf_op jit(solution)/shard_map/ppermute | solution.py:20
  1102.6 68.5 %collective-permute-done.10 = bf16[8,128,1536]{2,1,0:T(8,128)(2,1)} collective-permute-done((bf16[8,128,1536]{2,1,0:T(8,128)(2,1)}, bf16[8,128,1536]{2,1,0:T(8,128)(2,1)}, u32[]{:S(2)}, u32[]{:S(2)}) %collective-permute-start.10) | collective-permute-done | bytes 3145760 | tf_op jit(solution)/shard_map/ppermute | solution.py:20
  1171.1 11.7 collective-permute-done.9
  1182.8 4.7 collective-permute-done.7
  1187.5 9.9 add_convert_fusion.1
  1204.0 3.3 copy.117
  1207.4 10.7 fusion.65
  1219.9 10.2 fusion.62
  1232.0 5.0 fusion.46
  1237.3 107.5 %all-reduce.19 = (f32[768]{0:T(1024)S(1)}, f32[768]{0:T(1024)S(1)}, f32[768]{0:T(1024)S(1)}, f32[768]{0:T(1024)S(1)}, f32[768]{0:T(1024)S(1)}, /*index=5*/f32[30...) all-reduce(f32[768]{0:T(1024)S(1)} %reduce_sum.212, ...), channel_id=3, replica_groups=mesh['rows'=4,'seq'=8] {'rows','seq'}, use_global_device_ids=true, to_apply=%region_21.22.clone | all-reduce | flops 9216 | bytes 73728
  1350.1 6.7 add_add_fusion
  1356.8 78.1 %reduce-scatter.23.cloned.1.call-done = f32[24,768]{1,0:T(8,128)} async-done(((f32[768,768]{1,0:T(8,128)}), f32[24,768]{1,0:T(8,128)}) %reduce-scatter.23.cloned.1.call-update) | async-done | bytes 73744
  1434.9 104.3 %reduce-scatter.21.cloned.1.call-done = f32[24,768]{1,0:T(8,128)} async-done(((f32[768,768]{1,0:T(8,128)}), f32[24,768]{1,0:T(8,128)}) %reduce-scatter.21.cloned.1.call-update) | async-done | bytes 73744
  1539.2 142.0 %reduce-scatter.15.cloned.1.call-done = f32[24,3072]{1,0:T(8,128)} async-done(((f32[768,3072]{1,0:T(8,128)}), f32[24,3072]{1,0:T(8,128)}) %reduce-scatter.15.cloned.1.call-update) | async-done | bytes 294928 | tf_op jit(solution)/shard_map/reduce_scatter | solution.py:333
  1681.2 141.5 %reduce-scatter.17.cloned.1.call-done = f32[96,768]{1,0:T(8,128)} async-done(((f32[3072,768]{1,0:T(8,128)}), f32[96,768]{1,0:T(8,128)}) %reduce-scatter.17.cloned.1.call-update) | async-done | bytes 294928 | tf_op jit(solution)/shard_map/reduce_scatter | solution.py:335
  (355 shorter events, 274.2 us)
Async XLA Ops:
  7.2 60.7 %all-gather.7.cloned.1.call-start = ((), (), s32[]{:S(2)}) async-start(), calls=%async_computation.6 | async-start | bytes 1216512 | tf_op jit(solution)/shard_map/all_gather | solution.py:177
  7.9 116.1 %all-gather.9.cloned.1.call-start = ((), (), s32[]{:S(2)}) async-start(), calls=%async_computation.7 | async-start | bytes 1216512 | tf_op jit(solution)/shard_map/all_gather | solution.py:178
  8.7 402.8 %all-gather.11.cloned.1.call-start = ((), (), s32[]{:S(2)}) async-start(), calls=%async_computation.8 | async-start | bytes 1216512 | tf_op jit(solution)/shard_map/all_gather | solution.py:175
  9.4 505.1 %all-gather.13.cloned.1.call-start = ((), (), s32[]{:S(2)}) async-start(), calls=%async_computation.9 | async-start | bytes 1216512 | tf_op jit(solution)/shard_map/all_gather | solution.py:180
  10.0 569.7 %all-gather.15.cloned.1.call-start = ((), (), s32[]{:S(2)}) async-start(), calls=%async_computation.10 | async-start | bytes 4866048 | tf_op jit(solution)/shard_map/all_gather | solution.py:184
  10.6 633.8 %all-gather.17.cloned.1.call-start = ((), (), s32[]{:S(2)}) async-start(), calls=%async_computation.11 | async-start | bytes 4866048 | tf_op jit(solution)/shard_map/all_gather | solution.py:186
  131.5 6.5 copy-start.36
  134.4 125.3 %collective-permute-start = (bf16[8,128,1536]{1,2,0:T(8,128)(2,1)}, bf16[8,128,1536]{1,2,0:T(8,128)(2,1)S(1)}, u32[]{:S(2)}, u32[]{:S(2)}) collective-permute-start(bf16[8,128,1536]{1,2,0:T(8,128)(2,1)} %copy.94), channel_id=1, source_target_pairs={{0,3},{1,4},{2,5},{3,6},{4,7},{8,11},{9,12},{10,13},{11,14},{12,15... | collective-permute-start | bytes 9437192 | tf_op jit(solution)/shard_map/ppermute | solution.py:20
  138.0 1218.9 %reduce-scatter.13.cloned.1.call-start = ((), (), s32[]{:S(2)}) async-start(), calls=%async_computation.12 | async-start | bytes 2433024 | tf_op jit(solution)/shard_map/reduce_scatter | solution.py:329
  138.1 281.8 %collective-permute-start.1 = (bf16[8,128,1536]{1,2,0:T(8,128)(2,1)}, bf16[8,128,1536]{1,2,0:T(8,128)(2,1)}, u32[]{:S(2)}, u32[]{:S(2)}) collective-permute-start(bf16[8,128,1536]{1,2,0:T(8,128)(2,1)} %copy.94), channel_id=1, source_target_pairs={{0,2},{1,3},{2,4},{3,5},{4,6},{5,7},{8,10},{9,11},{10,12},{11,13},... | collective-permute-start | bytes 9437192 | tf_op jit(solution)/shard_map/ppermute | solution.py:20
  142.7 279.8 %collective-permute-start.2 = (bf16[8,128,1536]{1,2,0:T(8,128)(2,1)}, bf16[8,128,1536]{1,2,0:T(8,128)(2,1)}, u32[]{:S(2)}, u32[]{:S(2)}) collective-permute-start(bf16[8,128,1536]{1,2,0:T(8,128)(2,1)} %copy.94), channel_id=1, source_target_pairs={{0,1},{1,2},{2,3},{3,4},{4,5},{5,6},{6,7},{8,9},{9,10},{10,11},{11... | collective-permute-start | bytes 9437192 | tf_op jit(solution)/shard_map/ppermute | solution.py:20
  147.9 111.8 %copy-start.27 = (f32[768]{0:T(1024)}, f32[768]{0:T(1024)S(1)}, u32[]{:S(2)}) copy-start(f32[768]{0:T(1024)S(1)} %convert_element_type.163) | copy-start | bytes 9220
  152.2 275.7 %collective-permute-start.3 = (bf16[8,128,1536]{1,2,0:T(8,128)(2,1)}, bf16[8,128,1536]{1,2,0:T(8,128)(2,1)}, u32[]{:S(2)}, u32[]{:S(2)}) collective-permute-start(bf16[8,128,1536]{1,2,0:T(8,128)(2,1)} %copy.94), channel_id=1, source_target_pairs={{1,0},{2,1},{3,2},{4,3},{5,4},{6,5},{7,6},{9,8},{10,9},{11,10},{12... | collective-permute-start | bytes 9437192 | tf_op jit(solution)/shard_map/ppermute | solution.py:20
  153.5 277.0 %collective-permute-start.4 = (bf16[8,128,1536]{1,2,0:T(8,128)(2,1)}, bf16[8,128,1536]{1,2,0:T(8,128)(2,1)}, u32[]{:S(2)}, u32[]{:S(2)}) collective-permute-start(bf16[8,128,1536]{1,2,0:T(8,128)(2,1)} %copy.94), channel_id=1, source_target_pairs={{2,0},{3,1},{4,2},{5,3},{6,4},{7,5},{10,8},{11,9},{12,10},{13,11},... | collective-permute-start | bytes 9437192 | tf_op jit(solution)/shard_map/ppermute | solution.py:20
  259.7 3.2 copy-start.11
  259.7 173.6 %collective-permute-start.5 = (bf16[8,128,1536]{1,2,0:T(8,128)(2,1)}, bf16[8,128,1536]{1,2,0:T(8,128)(2,1)}, u32[]{:S(2)}, u32[]{:S(2)}) collective-permute-start(bf16[8,128,1536]{1,2,0:T(8,128)(2,1)} %copy.94), channel_id=1, source_target_pairs={{3,0},{4,1},{5,2},{6,3},{7,4},{11,8},{12,9},{13,10},{14,11},{15,12... | collective-permute-start | bytes 9437192 | tf_op jit(solution)/shard_map/ppermute | solution.py:20
  261.6 428.9 %copy-start.23 = (f32[768]{0:T(1024)}, f32[768]{0:T(1024)S(1)}, u32[]{:S(2)}) copy-start(f32[768]{0:T(1024)S(1)} %convert_element_type.157) | copy-start | bytes 9220
  261.6 382.7 %copy-start.25 = (f32[768]{0:T(1024)}, f32[768]{0:T(1024)S(1)}, u32[]{:S(2)}) copy-start(f32[768]{0:T(1024)S(1)} %convert_element_type.158) | copy-start | bytes 9220
  417.4 1.9 copy-start.12
  435.9 7.3 copy-start
  507.9 6.6 copy-start.4
  507.9 6.6 copy-start.10
  518.4 172.1 %copy-start.1 = (f32[1024,768]{1,0:T(8,128)}, f32[1024,768]{1,0:T(8,128)S(1)}, u32[]{:S(2)}) copy-start(f32[1024,768]{1,0:T(8,128)S(1)} %get-tuple-element.300) | copy-start | bytes 9437188
  518.4 172.1 %copy-start.19 = (f32[1024]{0:T(1024)}, f32[1024]{0:T(1024)S(1)}, u32[]{:S(2)}) copy-start(f32[1024]{0:T(1024)S(1)} %broadcast_multiply_fusion.4) | copy-start | bytes 12292
  518.9 171.6 %copy-start.21 = (f32[1024]{0:T(1024)}, f32[1024]{0:T(1024)S(1)}, u32[]{:S(2)}) copy-start(f32[1024]{0:T(1024)S(1)} %add_rsqrt_fusion.1) | copy-start | bytes 12292
  518.9 125.4 %copy-start.37 = (f32[768]{0:T(1024)S(1)}, f32[768]{0:T(1024)}, u32[]{:S(2)}) copy-start(f32[768]{0:T(1024)} %convert_element_type.162) | copy-start | bytes 9220
  653.1 1.9 copy-start.3
  653.2 1.9 copy-start.28
  655.0 1.6 copy-start.29
  655.0 1.6 copy-start.30
  690.5 3.5 copy-start.41
  692.2 1.7 copy-start.13
  696.2 1.4 copy-start.7
  923.3 114.5 %copy-start.8 = (bf16[8,128,12,64]{1,3,2,0:T(8,128)(2,1)}, bf16[8,128,12,64]{1,3,2,0:T(8,128)(2,1)S(1)}, u32[]{:S(2)}) copy-start(bf16[8,128,12,64]{1,3,2,0:T(8,128)(2,1)S(1)} %get-tuple-element.95) | copy-start | bytes 4718596
  947.3 14.9 copy-start.14
  947.3 14.9 copy-start.16
  960.8 75.5 %collective-permute-start.6 = (bf16[8,128,1536]{2,1,0:T(8,128)(2,1)}, bf16[8,128,1536]{2,1,0:T(8,128)(2,1)}, u32[]{:S(2)}, u32[]{:S(2)}) collective-permute-start(bf16[8,128,1536]{2,1,0:T(8,128)(2,1)} %get-tuple-element.289), channel_id=1, source_target_pairs={{3,0},{4,1},{5,2},{6,3},{7,4},{11,8},{12,9},{13,10},{14,11},{15,12... | collective-permute-start | bytes 9437192 | tf_op jit(solution)/shard_map/ppermute | solution.py:20
  964.9 391.9 %reduce-scatter.19.cloned.1.call-start = ((), (), s32[]{:S(2)}) async-start(), calls=%async_computation.15 | async-start | bytes 2433024
  965.0 137.6 %collective-permute-start.11 = (bf16[8,128,1536]{2,1,0:T(8,128)(2,1)}, bf16[8,128,1536]{2,1,0:T(8,128)(2,1)}, u32[]{:S(2)}, u32[]{:S(2)}) collective-permute-start(bf16[8,128,1536]{2,1,0:T(8,128)(2,1)} %get-tuple-element.290), channel_id=1, source_target_pairs={{0,3},{1,4},{2,5},{3,6},{4,7},{8,11},{9,12},{10,13},{11,14},{12,15... | collective-permute-start | bytes 9437192 | tf_op jit(solution)/shard_map/ppermute | solution.py:20
  972.1 199.0 %collective-permute-start.10 = (bf16[8,128,1536]{2,1,0:T(8,128)(2,1)}, bf16[8,128,1536]{2,1,0:T(8,128)(2,1)}, u32[]{:S(2)}, u32[]{:S(2)}) collective-permute-start(bf16[8,128,1536]{2,1,0:T(8,128)(2,1)} %get-tuple-element.291), channel_id=1, source_target_pairs={{0,2},{1,3},{2,4},{3,5},{4,6},{5,7},{8,10},{9,11},{10,12},{11,13},... | collective-permute-start | bytes 9437192 | tf_op jit(solution)/shard_map/ppermute | solution.py:20
  978.7 204.1 %collective-permute-start.9 = (bf16[8,128,1536]{2,1,0:T(8,128)(2,1)}, bf16[8,128,1536]{2,1,0:T(8,128)(2,1)}, u32[]{:S(2)}, u32[]{:S(2)}) collective-permute-start(bf16[8,128,1536]{2,1,0:T(8,128)(2,1)} %get-tuple-element.292), channel_id=1, source_target_pairs={{0,1},{1,2},{2,3},{3,4},{4,5},{5,6},{6,7},{8,9},{9,10},{10,11},{11... | collective-permute-start | bytes 9437192 | tf_op jit(solution)/shard_map/ppermute | solution.py:20
  983.2 199.7 %collective-permute-start.8 = (bf16[8,128,1536]{2,1,0:T(8,128)(2,1)}, bf16[8,128,1536]{2,1,0:T(8,128)(2,1)}, u32[]{:S(2)}, u32[]{:S(2)}) collective-permute-start(bf16[8,128,1536]{2,1,0:T(8,128)(2,1)} %get-tuple-element.293), channel_id=1, source_target_pairs={{1,0},{2,1},{3,2},{4,3},{5,4},{6,5},{7,6},{9,8},{10,9},{11,10},{12... | collective-permute-start | bytes 9437192 | tf_op jit(solution)/shard_map/ppermute | solution.py:20
  1036.4 151.2 %collective-permute-start.7 = (bf16[8,128,1536]{2,1,0:T(8,128)(2,1)}, bf16[8,128,1536]{2,1,0:T(8,128)(2,1)}, u32[]{:S(2)}, u32[]{:S(2)}) collective-permute-start(bf16[8,128,1536]{2,1,0:T(8,128)(2,1)} %get-tuple-element.294), channel_id=1, source_target_pairs={{2,0},{3,1},{4,2},{5,3},{6,4},{7,5},{10,8},{11,9},{12,10},{13,11},... | collective-permute-start | bytes 9437192 | tf_op jit(solution)/shard_map/ppermute | solution.py:20
  1045.0 152.4 %copy-start.40 = (bf16[8,128,768]{2,1,0:T(8,128)(2,1)S(1)}, bf16[8,128,768]{2,1,0:T(8,128)(2,1)}, u32[]{:S(2)}) copy-start(bf16[8,128,768]{2,1,0:T(8,128)(2,1)} %param.22) | copy-start | bytes 4718596
  1045.0 389.9 %reduce-scatter.23.cloned.1.call-start = ((), (), s32[]{:S(2)}) async-start(), calls=%async_computation.17 | async-start | bytes 2433024
  1197.4 2.7 copy-start.5
  1203.9 335.3 %reduce-scatter.21.cloned.1.call-start = ((), (), s32[]{:S(2)}) async-start(), calls=%async_computation.16 | async-start | bytes 2433024
  1203.9 3.4 copy-start.2
  1203.9 3.4 copy-start.20
  1203.9 3.4 copy-start.22
  1203.9 3.4 copy-start.24
  1204.0 3.4 copy-start.26
  1207.3 474.0 %reduce-scatter.15.cloned.1.call-start = ((), (), s32[]{:S(2)}) async-start(), calls=%async_computation.13 | async-start | bytes 9732096 | tf_op jit(solution)/shard_map/reduce_scatter | solution.py:333
  1218.0 1.9 copy-start.15
  1218.1 604.6 %reduce-scatter.17.cloned.1.call-start = ((), (), s32[]{:S(2)}) async-start(), calls=%async_computation.14 | async-start | bytes 9732096 | tf_op jit(solution)/shard_map/reduce_scatter | solution.py:335
  1230.2 1.4 copy-start.9
  1231.9 5.1 copy-start.6
  1231.9 5.3 copy-start.31
  1231.9 5.3 copy-start.32
  1231.9 5.4 copy-start.33
  1231.9 5.4 copy-start.34
  1231.9 5.4 copy-start.35
  1231.9 5.4 copy-start.38
  1232.0 5.4 copy-start.39
  (2 other events, 2.5 us)
Sparse Core Ops, SparseCore 0:
  10.9 56.9 all-gather.6
  70.8 53.1 all-gather.8
  127.0 284.4 all-gather.10
  414.2 100.2 all-gather.12
  517.3 62.3 all-gather.14
  582.5 61.8 all-gather.16
  965.1 260.7 reduce-scatter.12
  1231.7 98.4 reduce-scatter.18
  1336.1 98.7 reduce-scatter.22
  1440.6 98.5 reduce-scatter.20
  1545.7 135.5 reduce-scatter.14
  1687.6 135.0 reduce-scatter.16
where the time goes:
time: 1840 us; the launch traced here: 1830 us
  waiting for transfers between devices  1070 us (58%)
  matrix products  228 us (12%)
  local copies, waits for them, and re-layouts  226 us (12%)
  blocking collectives  150 us (8%)
  other arithmetic  100 us (5%)
  starting transfers between devices  40.4 us (2%)
    ppermute x12, waiting for transfers between devices, passed_along(): return lax.ppermute(block, axis, route)  299 us
    unnamed x15, waiting for transfers between devices  186 us
    unnamed x2, blocking collectives  150 us
    all_gather x1, waiting for transfers between devices, body(): lax.all_gather(shards[0], ('rows', 'seq'), axis=0, tiled=True)  148 us
    reduce_scatter x1, waiting for transfers between devices, body(): lax.psum_scatter(partial_grads[9], ('rows', 'seq'), scatter_dimension=0,...  142 us
    reduce_scatter x1, waiting for transfers between devices, body(): lax.psum_scatter(partial_grads[11], ('rows', 'seq'), scatter_dimension=0,...  141 us
    dynamic_update_slice x16, local copies, waits for them, and re-layouts, body(): lax.map(partial(attend_back, score_scale=score_scale), (query_b, window,...  92 us
    all_gather x1, waiting for transfers between devices, body(): lax.all_gather(shards[9], ('rows', 'seq'), axis=0, tiled=True)  60.8 us
  transfers between devices with their start and end apart: 24, of which 16 were waited for; matrix products, arithmetic and copies ran while one was open for 12% of the time, Pallas kernels for 0%

commit v1 on v0

--- a/solution.py
+++ b/solution.py
@@ -3,6 +3,8 @@
 import jax
 import jax.numpy as jnp
 from jax import lax
+from jax.experimental import pallas as pl
+from jax.experimental.pallas import tpu as pltpu
 from jax.sharding import PartitionSpec as P
 
 HEADS = 12
@@ -359,6 +361,588 @@
     )
 
 
+MESH = pl.DeviceIdType.MESH
+
+
+def place():
+    r = lax.axis_index("rows")
+    s = lax.axis_index("seq")
+    return r // 2, r % 2, s // 2, s % 2, r, s
+
+
+def greet(x, c, r, s, seq_size):
+    barrier = pltpu.get_barrier_semaphore()
+    for k in range(1, seq_size):
+        pl.semaphore_signal(
+            barrier, inc=1, device_id=(r, lax.rem(s + k, seq_size)), device_id_type=MESH
+        )
+    pl.semaphore_signal(barrier, inc=1, device_id=((1 - x) * 2 + c, s), device_id_type=MESH)
+    pl.semaphore_signal(barrier, inc=1, device_id=(x * 2 + 1 - c, s), device_id_type=MESH)
+    pl.semaphore_wait(barrier, seq_size + 1)
+
+
+def remote(src, dst, send, recv, device):
+    return pltpu.make_async_remote_copy(
+        src_ref=src, dst_ref=dst, send_sem=send, recv_sem=recv, device_id=device, device_id_type=MESH
+    )
+
+
+def column_view(ref, lo, width):
+    def view(x, c, z, y):
+        return ref.at[x, c, z, y, :, pl.ds(lo, width)]
+
+    return view
+
+
+def gather_kernel(
+    depth, seq_size, lanes, qkv_s, out_s, inner_s, outer_s, vec_s, x_in, cot_in,
+    qkv_g, out_g, inner_g, outer_g, vec_g, x_row, cot_row,
+    z_send, z_recv, p_send, p_recv, c_send, c_recv, e_send, e_recv, own_sem,
+):
+    x, c, z, y, r, s = place()
+    xo, co, yo = 1 - x, 1 - c, 1 - y
+    every = slice(None)
+    greet(x, c, r, s, seq_size)
+    pieces = []
+    for src, dst, lo, width, order in (
+        (qkv_s, qkv_g, 0, lanes[0] // 2, 0),
+        (qkv_s, qkv_g, lanes[0] // 2, lanes[0] // 2, 1),
+        (vec_s, vec_g, 0, 128, 0),
+        (out_s, out_g, 0, lanes[1] // 2, 0),
+        (out_s, out_g, lanes[1] // 2, lanes[1] // 2, 1),
+        (inner_s, inner_g, 0, lanes[2], 0),
+        (outer_s, outer_g, 0, lanes[1], 1),
+    ):
+        pieces.append((src.at[:, pl.ds(lo, width)], column_view(dst, lo, width), order))
+    count = len(pieces)
+    dev_x, dev_c, dev_y = (xo * 2 + c, s), (x * 2 + co, s), (r, z * 2 + yo)
+
+    def z_copy(i, k):
+        src, view, _ = pieces[i]
+        return remote(
+            src, view(x, c, z, y), z_send.at[i, k - 1], z_recv.at[i, k - 1],
+            (r, lax.rem(z + k, depth) * 2 + y),
+        )
+
+    def z_arrive(i, k):
+        src, view, _ = pieces[i]
+        return remote(
+            src, view(x, c, lax.rem(z + depth - k, depth), y), z_send.at[i, k - 1],
+            z_recv.at[i, k - 1], (r, s),
+        )
+
+    def second(i, mine):
+        view, order = pieces[i][1], pieces[i][2]
+        there = (view(x, c, every, y if mine else yo), view(x if mine else xo, c, every, y))[order]
+        return remote(there, there, p_send.at[i, 0], p_recv.at[i, 0], (dev_y, dev_x)[order])
+
+    def third(i, mine):
+        view, order = pieces[i][1], pieces[i][2]
+        there = (view(x if mine else xo, c, every, every), view(every, c, every, y if mine else yo))[order]
+        return remote(there, there, p_send.at[i, 1], p_recv.at[i, 1], (dev_x, dev_y)[order])
+
+    def cross(i, step, mine):
+        view, order = pieces[i][1], pieces[i][2]
+        cc = c if mine else co
+        there = (
+            (view(x, cc, every, y), view(x, cc, every, yo), view(xo, cc, every, every)),
+            (view(x, cc, every, y), view(xo, cc, every, y), view(every, cc, every, yo)),
+        )[order][step]
+        return remote(there, there, c_send.at[i, step], c_recv.at[i, step], dev_c)
+
+    def own(i):
+        src, view, _ = pieces[i]
+        return pltpu.make_async_copy(src, view(x, c, z, y), own_sem.at[i])
+
+    def row_copy(which, k, mine):
+        src, dst = ((x_in, x_row), (cot_in, cot_row))[which]
+        peer = lax.rem(s + k, seq_size)
+        slot = s if mine else lax.rem(s + seq_size - k, seq_size)
+        return remote(
+            src.at[peer], dst.at[slot], e_send.at[which, k - 1], e_recv.at[which, k - 1], (r, peer)
+        )
+
+    def row_own(which):
+        src, dst = ((x_in, x_row), (cot_in, cot_row))[which]
+        return pltpu.make_async_copy(src.at[s], dst.at[s], own_sem.at[count + which])
+
+    for i in range(2):
+        for k in range(1, depth):
+            z_copy(i, k).start()
+    for k in range(1, seq_size):
+        row_copy(0, k, True).start()
+    for i in range(2, count):
+        for k in range(1, depth):
+            z_copy(i, k).start()
+    for i in range(count):
+        own(i).start()
+    row_own(0).start()
+    for k in range(1, seq_size):
+        row_copy(1, k, True).start()
+    row_own(1).start()
+    for i in range(count):
+        own(i).wait()
+        for k in range(1, depth):
+            z_arrive(i, k).wait_recv()
+        second(i, True).start()
+        cross(i, 0, True).start()
+    for i in range(count):
+        second(i, False).wait_recv()
+        third(i, True).start()
+        cross(i, 1, True).start()
+    for i in range(count):
+        third(i, False).wait_recv()
+        cross(i, 2, True).start()
+    for which in range(2):
+        row_own(which).wait()
+        for k in range(1, seq_size):
+            row_copy(which, k, False).wait_recv()
+            row_copy(which, k, True).wait_send()
+    for i in range(count):
+        for step in range(3):
+            cross(i, step, False).wait_recv()
+            cross(i, step, True).wait_send()
+        for k in range(1, depth):
+            z_copy(i, k).wait_send()
+        second(i, True).wait_send()
+        third(i, True).wait_send()
+
+
+def gather_all(shards, layer_in, cotangent, depth, seq_size):
+    qkv, out, inner, outer, vec = shards
+    count = 7
+    shapes = [jax.ShapeDtypeStruct((2, 2, depth, 2) + a.shape, a.dtype) for a in shards]
+    rows = jax.ShapeDtypeStruct(layer_in.shape, layer_in.dtype)
+    hbm = pl.BlockSpec(memory_space=pl.ANY)
+    dma = pltpu.SemaphoreType.DMA
+    lanes = (qkv.shape[1], out.shape[1], inner.shape[1])
+    return pl.pallas_call(
+        partial(gather_kernel, depth, seq_size, lanes),
+        out_shape=tuple(shapes) + (rows, rows),
+        in_specs=[hbm] * 7,
+        out_specs=(hbm,) * 7,
+        scratch_shapes=[
+            dma((count, depth - 1)), dma((count, depth - 1)), dma((count, 2)), dma((count, 2)),
+            dma((count, 3)), dma((count, 3)), dma((2, seq_size - 1)), dma((2, seq_size - 1)),
+            dma((count + 2,)),
+        ],
+        compiler_params=pltpu.CompilerParams(collective_id=0, has_side_effects=True),
+        name="gather_all",
+    )(qkv, out, inner, outer, vec, layer_in, cotangent)
+
+
+def reduce_kernel(
+    depth, seq_size, lanes, qkv_p, out_p, inner_p, outer_p, vec_p, lo_in, gi_in,
+    qkv_r, out_r, inner_r, outer_r, vec_r, lo_row, gi_row, *scratch,
+):
+    x, c, z, y, r, s = place()
+    xo, co, yo = 1 - x, 1 - c, 1 - y
+    every = slice(None)
+    count = 7
+    first, middle, last = scratch[:5], scratch[5:12], scratch[12:17]
+    tail = scratch[17:22]
+    c_send, c_recv, p_send, p_recv, z_send, z_recv, e_send, e_recv, own_sem = scratch[22:]
+    greet(x, c, r, s, seq_size)
+    dev_x, dev_c, dev_y = (xo * 2 + c, s), (x * 2 + co, s), (r, z * 2 + yo)
+    pieces = []
+    for a, (src, lo, width, order) in enumerate((
+        (0, 0, lanes[0] // 2, 0),
+        (0, lanes[0] // 2, lanes[0] // 2, 1),
+        (1, 0, lanes[1] // 2, 0),
+        (1, lanes[1] // 2, lanes[1] // 2, 1),
+        (2, 0, lanes[2], 0),
+        (3, 0, lanes[1], 1),
+        (4, 0, 128, 0),
+    )):
+        pieces.append((src, pl.ds(lo, width), order))
+    partials = (qkv_p, out_p, inner_p, outer_p, vec_p)
+    results = (qkv_r, out_r, inner_r, outer_r, vec_r)
+
+    def cross(i):
+        a, cols, _ = pieces[i]
+        return remote(
+            partials[a].at[:, co, :, :, :, cols], first[a].at[:, :, :, :, cols],
+            c_send.at[i], c_recv.at[i], dev_c,
+        )
+
+    def second(i):
+        a, cols, order = pieces[i]
+        held = first[a]
+        src = (held.at[xo, :, :, :, cols], held.at[:, :, yo, :, cols])[order]
+        return remote(src, middle[i], p_send.at[i, 0], p_recv.at[i, 0], (dev_x, dev_y)[order])
+
+    def third(i):
+        a, cols, order = pieces[i]
+        held = first[a]
+        src = (held.at[x, :, yo, :, cols], held.at[xo, :, y, :, cols])[order]
+        return remote(src, last[a].at[:, :, cols], p_send.at[i, 1], p_recv.at[i, 1], (dev_y, dev_x)[order])
+
+    def along(i, k):
+        a, cols, _ = pieces[i]
+        zt = lax.rem(z + k, depth)
+        return remote(
+            first[a].at[x, zt, y, :, cols], tail[a].at[k - 1, :, cols],
+            z_send.at[i, k - 1], z_recv.at[i, k - 1], (r, zt * 2 + y),
+        )
+
+    def add(dst, a_val, b_val):
+        return (a_val.astype(jnp.float32) + b_val.astype(jnp.float32)).astype(dst.dtype)
+
+    def row_copy(which, k, mine):
+        src, dst = ((lo_in, lo_row), (gi_in, gi_row))[which]
+        peer = lax.rem(s + k, seq_size)
+        slot = s if mine else lax.rem(s + seq_size - k, seq_size)
+        return remote(
+            src.at[peer], dst.at[slot], e_send.at[which, k - 1], e_recv.at[which, k - 1], (r, peer)
+        )
+
+    def row_own(which):
+        src, dst = ((lo_in, lo_row), (gi_in, gi_row))[which]
+        return pltpu.make_async_copy(src.at[s], dst.at[s], own_sem.at[which])
+
+    sequence = (4, 5, 0, 1, 2, 3, 6)
+    for i in sequence:
+        cross(i).start()
+    for which in range(2):
+        row_own(which).start()
+        for k in range(1, seq_size):
+            row_copy(which, k, True).start()
+    for i in sequence:
+        a, cols, order = pieces[i]
+        cross(i).wait_recv()
+
+        @pl.loop(0, 4 * depth)
+        def _(n, a=a, cols=cols):
+            n0, n1, n2 = n // (2 * depth), (n // 2) % depth, n % 2
+            first[a][n0, n1, n2, :, cols] = add(
+                first[a], first[a][n0, n1, n2, :, cols], partials[a][n0, c, n1, n2, :, cols]
+            )
+
+        second(i).start()
+    for i in sequence:
+        a, cols, order = pieces[i]
+        second(i).wait_recv()
+
+        @pl.loop(0, 2 * depth)
+        def _(n, i=i, a=a, cols=cols, order=order):
+            n0, n1 = n // 2, n % 2
+            if order == 0:
+                at = (x, n0, n1, slice(None), cols)
+                come = (n0, n1)
+            else:
+                at = (n1, n0, y, slice(None), cols)
+                come = (n1, n0)
+            first[a][at] = add(first[a], first[a][at], middle[i][come])
+
+        third(i).start()
+    for i in sequence:
+        a, cols, order = pieces[i]
+        third(i).wait_recv()
+
+        @pl.loop(0, depth)
+        def _(n, a=a, cols=cols):
+            at = (x, n, y, slice(None), cols)
+            first[a][at] = add(first[a], first[a][at], last[a][n, :, cols])
+
+        for k in range(1, depth):
+            along(i, k).start()
+    for i in sequence:
+        a, cols, order = pieces[i]
+        total = first[a][x, z, y, :, cols].astype(jnp.float32)
+        for k in range(1, depth):
+            along(i, k).wait_recv()
+            total = total + tail[a][k - 1, :, cols].astype(jnp.float32)
+        results[a][:, cols] = total
+    for which in range(2):
+        row_own(which).wait()
+        for k in range(1, seq_size):
+            row_copy(which, k, False).wait_recv()
+            row_copy(which, k, True).wait_send()
+    for i in sequence:
+        cross(i).wait_send()
+        second(i).wait_send()
+        third(i).wait_send()
+        for k in range(1, depth):
+            along(i, k).wait_send()
+
+
+def reduce_all(partials, layer_out, grad_in, depth, seq_size):
+    count = 7
+    hbm = pl.BlockSpec(memory_space=pl.ANY)
+    vmem = pl.BlockSpec(memory_space=pltpu.VMEM)
+    dma = pltpu.SemaphoreType.DMA
+    lanes = (partials[0].shape[-1], partials[1].shape[-1], partials[2].shape[-1])
+    blocks = [(p.shape[-2:], p.dtype) for p in partials]
+    scratch = [pltpu.VMEM((2, depth, 2) + b, t) for b, t in blocks]
+    for a, width, order in (
+        (0, lanes[0] // 2, 0), (0, lanes[0] // 2, 1), (1, lanes[1] // 2, 0), (1, lanes[1] // 2, 1),
+        (2, lanes[2], 0), (3, lanes[1], 1), (4, 128, 0),
+    ):
+        lead = ((depth, 2), (2, depth))[order]
+        scratch.append(pltpu.VMEM(lead + (blocks[a][0][0], width), blocks[a][1]))
+    scratch += [pltpu.VMEM((depth,) + b, t) for b, t in blocks]
+    scratch += [pltpu.VMEM((depth - 1,) + b, t) for b, t in blocks]
+    return pl.pallas_call(
+        partial(reduce_kernel, depth, seq_size, lanes),
+        out_shape=tuple(jax.ShapeDtypeStruct(b, jnp.float32) for b, _ in blocks)
+        + (jax.ShapeDtypeStruct(layer_out.shape, layer_out.dtype), jax.ShapeDtypeStruct(grad_in.shape, grad_in.dtype)),
+        in_specs=[vmem] * 5 + [hbm] * 2,
+        out_specs=(vmem,) * 5 + (hbm,) * 2,
+        scratch_shapes=scratch + [
+            dma((count,)), dma((count,)), dma((count, 2)), dma((count, 2)),
+            dma((count, depth - 1)), dma((count, depth - 1)),
+            dma((2, seq_size - 1)), dma((2, seq_size - 1)), dma((2,)),
+        ],
+        compiler_params=pltpu.CompilerParams(
+            collective_id=1, has_side_effects=True, vmem_limit_bytes=60 * 1024 * 1024
+        ),
+        name="reduce_all",
+    )(*partials, layer_out, grad_in)
+
+
+FIRST_TILES = ((0, 128, 0, 512), (128, 128, 0, 576), (256, 128, 0, 576), (384, 128, 0, 576), (512, 64, 128, 448))
+LAST_TILES = ((576, 128, 576, 384), (704, 128, 576, 384), (832, 128, 576, 384))
+TILES = FIRST_TILES + LAST_TILES
+REAL = 960
+
+
+def both_heads(block):
+    low = lax.broadcasted_iota(jnp.int32, block.shape, 1) < HEAD_DIM
+    zero = jnp.zeros_like(block)
+    return jnp.concatenate([jnp.where(low, block, zero), jnp.where(low, zero, block)], axis=0)
+
+
+def pick_heads(wide, count):
+    low = lax.broadcasted_iota(jnp.int32, (2 * HEAD_DIM, count), 0) < HEAD_DIM
+    return jnp.where(low, wide[:, :count], wide[:, count:])
+
+
+def tile_scores(q_both, keys, seg_col, seg_row, tile, masked):
+    q0, qn, k0, kn = tile
+    scores = lax.dot_general(
+        keys, q_both, (((1,), (1,)), ((), ())), preferred_element_type=jnp.float32
+    )
+    if masked:
+        queries = seg_row[:, q0 : q0 + qn]
+        queries = jnp.concatenate([queries, queries], axis=1)
+        scores = jnp.where(seg_col[k0 : k0 + kn, :] == queries, scores, masked_score)
+    return scores
+
+
+def attend_kernel(q_ref, k_ref, v_ref, seg_col, seg_row, ctx_ref, lse_ref):
+    for n, tile in enumerate(TILES):
+        q0, qn, k0, kn = tile
+        q_both = both_heads(q_ref[q0 : q0 + qn, :] * jnp.bfloat16(HEAD_DIM**-0.5))
+        scores = tile_scores(q_both, k_ref[k0 : k0 + kn, :], seg_col, seg_row, tile, n < 5)
+        top = jnp.max(scores, axis=0, keepdims=True)
+        weights = jnp.exp(scores - top)
+        total = jnp.sum(weights, axis=0, keepdims=True)
+        probs = (weights * (1.0 / total)).astype(jnp.bfloat16)
+        lse_ref[0, n : n + 1, : 2 * qn] = top + jnp.log(total)
+        wide = lax.dot_general(
+            v_ref[k0 : k0 + kn, :], probs, (((0,), (0,)), ((), ())), preferred_element_type=jnp.float32
+        )
+        ctx_ref[q0 : q0 + qn, :] = pick_heads(wide, qn).T.astype(jnp.bfloat16)
+    ctx_ref[REAL:, :] = v_ref[REAL:, :]
+
+
+def attend(qkv, seg_col, seg_row):
+    tokens, features = qkv.shape[0], qkv.shape[1] // 3
+    pairs = features // 128
+
+    def part(j):
+        return pl.BlockSpec((tokens, 128), lambda p, j=j: (0, j * pairs + p))
+
+    whole = lambda shape: pl.BlockSpec(shape, lambda p: (0,) * len(shape))
+    return pl.pallas_call(
+        attend_kernel,
+        grid=(pairs,),
+        out_shape=(
+            jax.ShapeDtypeStruct((tokens, features), jnp.bfloat16),
+            jax.ShapeDtypeStruct((pairs, 8, 256), jnp.float32),
+        ),
+        in_specs=[part(0), part(1), part(2), whole((tokens, 1)), whole((1, tokens))],
+        out_specs=(
+            pl.BlockSpec((tokens, 128), lambda p: (0, p)),
+            pl.BlockSpec((1, 8, 256), lambda p: (p, 0, 0)),
+        ),
+        name="attend",
+    )(qkv, qkv, qkv, seg_col, seg_row)
+
+
+def attend_back_kernel(q_ref, k_ref, v_ref, g_ref, lse_ref, seg_col, seg_row, d_ref, dk_acc, dv_acc):
+    features = d_ref.shape[1] // 3
+    dk_acc[...] = jnp.zeros_like(dk_acc)
+    dv_acc[...] = jnp.zeros_like(dv_acc)
+    base = pl.program_id(0) * 128
+    q_cols = pl.ds(pl.multiple_of(base, 128), 128)
+    k_cols = pl.ds(pl.multiple_of(base + features, 128), 128)
+    v_cols = pl.ds(pl.multiple_of(base + 2 * features, 128), 128)
+    scale = HEAD_DIM**-0.5
+    for n, tile in enumerate(TILES):
+        q0, qn, k0, kn = tile
+        keys, values = k_ref[k0 : k0 + kn, :], v_ref[k0 : k0 + kn, :]
+        q_both = both_heads(q_ref[q0 : q0 + qn, :] * jnp.bfloat16(scale))
+        g_both = both_heads(g_ref[q0 : q0 + qn, :])
+        scores = tile_scores(q_both, keys, seg_col, seg_row, tile, n < 5)
+        probs = jnp.exp(scores - lse_ref[0, n : n + 1, : 2 * qn])
+        grad_probs = lax.dot_general(
+            values, g_both, (((1,), (1,)), ((), ())), preferred_element_type=jnp.float32
+        )
+        dots = jnp.sum(probs * grad_probs, axis=0, keepdims=True)
+        grad_scores = (probs * (grad_probs - dots)).astype(jnp.bfloat16)
+        dv_acc[k0 : k0 + kn, :] += jnp.dot(
+            probs.astype(jnp.bfloat16), g_both, preferred_element_type=jnp.float32
+        )
+        dk_acc[k0 : k0 + kn, :] += jnp.dot(grad_scores, q_both, preferred_element_type=jnp.float32)
+        wide = lax.dot_general(
+            keys, grad_scores, (((0,), (0,)), ((), ())), preferred_element_type=jnp.float32
+        )
+        d_ref[q0 : q0 + qn, q_cols] = (pick_heads(wide, qn).T * scale).astype(jnp.bfloat16)
+    d_ref[:REAL, k_cols] = dk_acc[...].astype(jnp.bfloat16)
+    d_ref[:REAL, v_cols] = dv_acc[...].astype(jnp.bfloat16)
+    pad = g_ref[REAL:, :]
+    d_ref[REAL:, q_cols] = jnp.zeros_like(pad)
+    d_ref[REAL:, k_cols] = jnp.zeros_like(pad)
+    d_ref[REAL:, v_cols] = pad
+
+
+def attend_grad(qkv, grad_context, lse, seg_col, seg_row):
+    tokens, features = grad_context.shape
+    pairs = features // 128
+
+    def part(j):
+        return pl.BlockSpec((tokens, 128), lambda p, j=j: (0, j * pairs + p))
+
+    whole = lambda shape: pl.BlockSpec(shape, lambda p: (0,) * len(shape))
+    return pl.pallas_call(
+        attend_back_kernel,
+        grid=(pairs,),
+        out_shape=jax.ShapeDtypeStruct((tokens, 3 * features), jnp.bfloat16),
+        in_specs=[
+            part(0), part(1), part(2), part(0), pl.BlockSpec((1, 8, 256), lambda p: (p, 0, 0)),
+            whole((tokens, 1)), whole((1, tokens)),
+        ],
+        out_specs=whole((tokens, 3 * features)),
+        scratch_shapes=[pltpu.VMEM((REAL, 128), jnp.float32), pltpu.VMEM((REAL, 128), jnp.float32)],
+        name="attend_grad",
+    )(qkv, qkv, qkv, grad_context, lse, seg_col, seg_row)
+
+
+def gelu_parts(u):
+    cdf = 0.5 * (1.0 + lax.erf(u * (2.0**-0.5)))
+    density = jnp.exp(-0.5 * u * u) * ((2.0 * jnp.pi) ** -0.5)
+    return u * cdf, cdf + u * density
+
+
+def row_body(
+    layer_in, cotangent, seg_lengths, query_weight, query_bias, key_weight, value_weight, value_bias,
+    out_weight, out_bias, attn_gain, attn_shift, inner_weight, inner_bias, outer_weight, outer_bias,
+    final_gain, final_shift,
+):
+    f32, bf16 = jnp.float32, jnp.bfloat16
+    row_count, block_len, features = layer_in.shape
+    seq_size = lax.axis_size("seq")
+    depth = seq_size // 2
+    devices = seq_size * lax.axis_size("rows")
+    tokens = row_count * block_len
+    hidden_units = inner_weight.shape[1]
+    narrow = query_bias.shape[0]
+    vectors = (
+        query_bias, value_bias, out_bias, attn_gain, attn_shift, outer_bias, final_gain, final_shift, inner_bias,
+    )
+    packed = jnp.concatenate(vectors)
+    packed = jnp.pad(packed, (0, 1024 - packed.shape[0])).reshape(8, 128)
+    shards = (
+        jnp.concatenate([query_weight, key_weight, value_weight], axis=1),
+        out_weight, inner_weight, outer_weight, packed,
+    )
+    qkv_g, out_g, inner_g, outer_g, vec_g, x_row, cot_row = gather_all(
+        shards, layer_in, cotangent, depth, seq_size
+    )
+    qkv_mat = qkv_g.reshape(features, 3 * features)
+    out_mat = out_g.reshape(features, features)
+    inner_mat = inner_g.reshape(features, hidden_units)
+    outer_mat = outer_g.reshape(hidden_units, features)
+    flat = vec_g.reshape(devices, 1024).astype(f32)
+    vecs = [flat[:, j * narrow : (j + 1) * narrow].reshape(features) for j in range(8)]
+    query_vec, value_vec, out_vec, attn_g, attn_s, outer_vec, final_g, final_s = vecs
+    inner_vec = flat[:, 8 * narrow : 8 * narrow + 4 * narrow].reshape(hidden_units)
+
+    inputs = x_row.reshape(tokens, features)
+    cot = cot_row.reshape(tokens, features)
+    lengths = lax.dynamic_index_in_dim(seg_lengths, lax.axis_index("seq"), 0, keepdims=False)
+    ends = jnp.cumsum(lengths)
+    positions = jnp.arange(tokens, dtype=jnp.int32)
+    seg_ids = jnp.sum((positions[:, None] >= ends[None, :]).astype(jnp.int32), axis=1)
+    real = (positions < ends[-1]).astype(f32)
+
+    qkv_vec = jnp.concatenate([query_vec, jnp.zeros_like(query_vec), value_vec])
+    qkv = (jnp.dot(inputs, qkv_mat, preferred_element_type=f32) + qkv_vec).astype(bf16)
+    context, lse = attend(qkv, seg_ids[:, None], seg_ids[None, :])
+    first_sum = inputs.astype(f32) + jnp.dot(context, out_mat, preferred_element_type=f32) + out_vec
+    normed_one, inv_std_one = norm_parts(first_sum)
+    hidden = normed_one * attn_g + attn_s
+    hidden_b = hidden.astype(bf16)
+    inner_pre = jnp.dot(hidden_b, inner_mat, preferred_element_type=f32) + inner_vec
+    active, slope = gelu_parts(inner_pre)
+    active, slope = active.astype(bf16), slope.astype(bf16)
+    outer_out = jnp.dot(active, outer_mat, preferred_element_type=f32) + outer_vec
+    normed_two, inv_std_two = norm_parts(hidden + outer_out)
+    layer_out = (normed_two * final_g + final_s).astype(bf16)
+
+    upstream = cot.astype(f32) * real[:, None]
+    grad_final_gain = jnp.sum(upstream * normed_two, axis=0)
+    grad_final_shift = jnp.sum(upstream, axis=0)
+    grad_second = norm_back(upstream, normed_two, inv_std_two, final_g)
+    grad_outer = grad_second.astype(bf16)
+    grad_outer_bias = jnp.sum(grad_outer.astype(f32), axis=0)
+    grad_outer_weight = jnp.einsum("tf,td->fd", active, grad_outer, preferred_element_type=f32)
+    grad_active = jnp.einsum("td,fd->tf", grad_outer, outer_mat, preferred_element_type=f32)
+    grad_inner = (grad_active * slope.astype(f32)).astype(bf16)
+    grad_inner_bias = jnp.sum(grad_inner.astype(f32), axis=0)
+    grad_inner_weight = jnp.einsum("td,tf->df", hidden_b, grad_inner, preferred_element_type=f32)
+    grad_hidden = grad_second + jnp.einsum("tf,df->td", grad_inner, inner_mat, preferred_element_type=f32)
+    grad_attn_gain = jnp.sum(grad_hidden * normed_one, axis=0)
+    grad_attn_shift = jnp.sum(grad_hidden, axis=0)
+    grad_first = norm_back(grad_hidden, normed_one, inv_std_one, attn_g)
+    grad_attended = grad_first.astype(bf16)
+    grad_out_bias = jnp.sum(grad_attended.astype(f32), axis=0)
+    grad_out_weight = jnp.einsum("td,te->de", context, grad_attended, preferred_element_type=f32)
+    grad_context = jnp.einsum("te,de->td", grad_attended, out_mat, preferred_element_type=f32).astype(bf16)
+    grad_qkv = attend_grad(qkv, grad_context, lse, seg_ids[:, None], seg_ids[None, :])
+    grad_qkv_weight = jnp.einsum("td,te->de", inputs, grad_qkv, preferred_element_type=f32)
+    grad_qkv_bias = jnp.sum(grad_qkv.astype(f32), axis=0)
+    grad_in = grad_first + jnp.einsum("te,de->td", grad_qkv, qkv_mat, preferred_element_type=f32)
+
+    narrow_grads = (
+        grad_qkv_bias[:features], grad_qkv_bias[2 * features :], grad_out_bias, grad_attn_gain,
+        grad_attn_shift, grad_outer_bias, grad_final_gain, grad_final_shift, grad_inner_bias,
+    )
+    vec_p = jnp.concatenate([v.reshape(devices, -1) for v in narrow_grads], axis=1)
+    vec_p = jnp.pad(vec_p, ((0, 0), (0, 1024 - vec_p.shape[1])))
+    lead = (2, 2, depth, 2)
+    partials = (
+        grad_qkv_weight.astype(bf16).reshape(lead + (-1, 3 * features)),
+        grad_out_weight.astype(bf16).reshape(lead + (-1, features)),
+        grad_inner_weight.astype(bf16).reshape(lead + (-1, hidden_units)),
+        grad_outer_weight.astype(bf16).reshape(lead + (-1, features)),
+        vec_p.reshape(lead + (8, 128)),
+    )
+    blocks = (row_count, block_len, features)
+    qkv_r, out_r, inner_r, outer_r, vec_r, layer_out, grad_in = reduce_all(
+        partials, layer_out.reshape(blocks), grad_in.astype(bf16).reshape(blocks), depth, seq_size
+    )
+    owned = vec_r.reshape(1024)
+    g_qb, g_vb, g_ob, g_ag, g_as, g_tb, g_fg, g_fs = [owned[j * narrow : (j + 1) * narrow] for j in range(8)]
+    g_ib = owned[8 * narrow : 12 * narrow]
+    return (
+        layer_out, grad_in.astype(f32),
+        qkv_r[:, :features], g_qb, qkv_r[:, features : 2 * features], qkv_r[:, 2 * features :], g_vb,
+        out_r, g_ob, g_ag, g_as, inner_r, g_ib, outer_r, g_tb, g_fg, g_fs,
+    )
+
+
 def solution(mesh):
     placed = (
         P("rows", "seq", None),
@@ -380,8 +964,9 @@
         P(("rows", "seq")),
         P(("rows", "seq")),
     )
+    by_row = mesh.shape["rows"] == 4 and mesh.shape["seq"] == 8
     return jax.shard_map(
-        body,
+        row_body if by_row else body,
         mesh=mesh,
         in_specs=placed,
         out_specs=(

time: 1840 us -> 471 us (0.26)
  waiting for transfers between devices: 1070 us -> 0 us
  Pallas kernels: 0 us -> 340 us
  local copies, waits for them, and re-layouts: 226 us -> 17.1 us
  blocking collectives: 150 us -> 0 us
  matrix products: 228 us -> 92.3 us
  other arithmetic: 100 us -> 15.3 us
  starting transfers between devices: 40.4 us -> 0 us
    pallas_call x0 -> x4, Pallas kernels: none -> 340 us  [the longest x1 152 us: gather_all(): pl.pallas_call(partial(gather_kernel, depth, seq_size, lanes), out_shape=...]
    all_gather x6 -> x0, waiting for transfers between devices: 302 us -> none  [the longest x1 148 us: body(): lax.all_gather(shards[0], ('rows', 'seq'), axis=0, tiled=True)]
    ppermute x12 -> x0, waiting for transfers between devices: 299 us -> none  [passed_along(): return lax.ppermute(block, axis, route)]
    reduce_scatter x3 -> x0, waiting for transfers between devices: 283 us -> none  [the longest x1 142 us: body(): lax.psum_scatter(partial_grads[9], ('rows', 'seq'), scatter_dimension=0,...]
    unnamed x15 -> x0, waiting for transfers between devices: 186 us -> none
    unnamed x2 -> x0, blocking collectives: 150 us -> none
    dot_general x71 -> x12, matrix products: 228 us -> 92.3 us  [the longest x1 13.3 us: row_body(): jnp.einsum('td,fd->tf', grad_outer, outer_mat, preferred_element_type=f32)]
    dynamic_update_slice x16 -> x0, local copies, waits for them, and re-layouts: 92 us -> none  [body(): lax.map(partial(attend_back, score_scale=score_scale), (query_b, window,...]
  transfers between devices with their start and end apart: 24 -> 0, of which waited for: 16 -> 0; matrix products, arithmetic and copies ran while one was open for 12% -> 0% of each run, Pallas kernels for 0% -> 0%
where the time goes in v1:
time: 471 us; the launch traced here: 466 us
  Pallas kernels  340 us (72%)
  matrix products  92.3 us (20%)
  local copies, waits for them, and re-layouts  17.1 us (4%)
  other arithmetic  15.3 us (3%)
    pallas_call x1, Pallas kernels, gather_all(): pl.pallas_call(partial(gather_kernel, depth, seq_size, lanes), out_shape=...  152 us
    pallas_call x1, Pallas kernels, reduce_all(): pl.pallas_call(partial(reduce_kernel, depth, seq_size, lanes), out_shape=...  138 us
    pallas_call x1, Pallas kernels, attend_grad(): pl.pallas_call(attend_back_kernel, grid=(pairs,), out_shape=jax.ShapeDtyp...  27.2 us
    pallas_call x1, Pallas kernels, attend(): pl.pallas_call(attend_kernel, grid=(pairs,), out_shape=(jax.ShapeDtypeStr...  22.5 us
    dot_general x1, matrix products, row_body(): jnp.einsum('td,fd->tf', grad_outer, outer_mat, preferred_element_type=f32)  13.3 us
    dot_general x1, matrix products, row_body(): jnp.dot(hidden_b, inner_mat, preferred_element_type=f32) + inner_vec  12.5 us
    dot_general x1, matrix products, row_body(): jnp.einsum('td,tf->df', hidden_b, grad_inner, preferred_element_type=f32)  10 us
    dot_general x1, matrix products, row_body(): jnp.einsum('tf,td->fd', active, grad_outer, preferred_element_type=f32)  9.83 us

profile of v1, /device:TPU:0, one launch (start us, length us, event | category | flops | bytes accessed | tf_op | source)
XLA Modules:
  0.0 466.3 jit_solution(902074416684746246)
XLA Ops:
  0.7 1.5 pad_maximum_fusion.qkv_s
  2.1 6.1 %concatenate.13 = bf16[288]{0:T(512)(128)(2,1)S(1)} concatenate(bf16[24]{0:T(256)(128)(2,1)} %param.22, bf16[24]{0:T(256)(128)(2,1)} %param.25, bf16[24]{0:T(256)(128)(2,1)} %param.27, bf16[24]{0:T(256)(128)(2,1)} %param.28, bf16[24]{0:T(256)(128)(2,1)} %param.29, bf16[24]{0:T(256)(128)(2,1)} %param.33, bf16[24]{0:T(256)(128)(2,1)} %param.34, bf16[24]{0:T(256)(128)(2,1)} %param.35, ...), dimensions={0} | concatenate | bytes 1152 | tf_op jit(solution)/shard_map/concatenate | solution.py:854
  8.2 0.6 pad_bitcast_fusion.1.vec_s
  8.8 152.3 %gather_all.1 = (bf16[2,2,4,2,24,2304]{5,4,3,2,1,0:T(8,128)(2,1)}, bf16[2,2,4,2,24,768]{5,4,3,2,1,0:T(8,128)(2,1)}, bf16[2,2,4,2,24,3072]{5,4,3,2,1,0:T(8,128)(2...) custom-call(bf16[24,2304]{1,0:T(8,128)(2,1)} %pad_maximum_fusion.qkv, ...), custom_call_target="tpu_custom_call" | custom-call | tf_op jit(solution)/shard_map/gather_all/pallas_call | solution.py:519
  161.1 0.9 copy.42
  162.0 0.1 fusion.18
  162.1 0.1 reshape.218
  162.1 0.1 reshape.219
  162.3 8.6 %add_convert_fusion.q_ref.k_ref.v_ref = bf16[1024,2304]{1,0:T(8,128)(2,1)} fusion(bf16[1024,768]{1,0:T(8,128)(2,1)} %bitcast.89, bf16[768,2304]{1,0:T(8,128)(2,1)} %bitcast.87, f32[2304]{0:T(1024)S(1)} %pad_maximum_fusion.1), kind=kOutput, calls=%fused_computation.11 | convolution fusion | flops 3628597248 | bytes 9839616 | tf_op jit(solution)/shard_map/dot_general | solution.py:881
  170.8 0.2 dynamic-slice_reduce_fusion
  171.0 0.2 reduce-window.4
  171.2 0.1 convert_reduce_fusion.4
  171.3 1.0 copy.37.seg_col
  172.3 22.5 %attend.1 = (bf16[1024,768]{1,0:T(8,128)(2,1)}, f32[6,8,256]{2,1,0:T(8,128)}) custom-call(bf16[1024,2304]{1,0:T(8,128)(2,1)} %add_convert_fusion.q_ref.k_ref.v_ref, bf16[1024,2304]{1,0:T(8,128)(2,1)} %add_convert_fusion.q_ref.k_ref.v_ref, bf16[1024,2304]{1,0:T(8,128)(2,1)} %add_convert_fusion.q_ref.k_ref.v_ref, s32[1024,1]{1,0:T(8,128)} %copy.37.seg_col, ...), custom_call_target="tpu_custom_call" | custom-call | tf_op jit(solution)/shard_map/attend/pallas_call | solution.py:757
  194.8 0.1 add.108
  194.9 3.8 fusion.21
  198.7 0.5 multiply_reduce_fusion.6
  199.2 0.1 mul.152
  199.3 0.1 add.112
  199.4 0.1 slice.118
  199.5 12.5 %multiply_convert_fusion.1 = (bf16[1024,3072]{1,0:T(8,128)(2,1)}, f32[1024,3072]{1,0:T(8,128)}) fusion(f32[3072]{0:T(1024)S(1)} %add.115, bf16[768,3072]{1,0:T(8,128)(2,1)} %bitcast.79, f32[1024,768]{1,0:T(8,128)S(1)} %get-tuple-element.84, f32[768]{0:T(1024)S(1)} %add.112, f32[768]{0:T(1024)S(1)} %mul.152, f32[1024]{0:T(1024)S(1)} %add_rsqrt_fusion.1, ...), kind=kOutput, calls=%fused_computation.8 | convolution fusion | flops 4854644736 | bytes 26765312 | tf_op jit(solution)/shard_map/dot_general | solution.py:887
  212.0 0.1 add.120
  212.1 9.4 %fusion.22 = (f32[1024]{0:T(1024)S(1)}, f32[1024,768]{1,0:T(8,128)S(1)}) fusion(f32[768]{0:T(1024)S(1)} %add.120, bf16[1024,3072]{1,0:T(8,128)(2,1)} %get-tuple-element.85, bf16[3072,768]{1,0:T(8,128)(2,1)} %bitcast.83, f32[768]{0:T(1024)S(1)} %add.112, f32[768]{0:T(1024)S(1)} %mul.152, f32[1024]{0:T(1024)S(1)} %add_rsqrt_fusion.1, ...), kind=kOutput, calls=%fused_computation.72 | convolution fusion | flops 4837342208 | bytes 17323008 | tf_op jit(solution)/shard_map/dot_general | solution.py:890
  221.5 0.5 multiply_reduce_fusion.5
  222.0 0.1 mul.164
  222.1 0.1 add.127
  222.2 0.6 slice.96
  222.8 0.6 fusion.9
  223.5 3.9 multiply_reduce_fusion
  227.4 0.7 fusion.8
  228.1 0.7 fusion.6
  228.8 1.3 convert_reduce_fusion.2
  230.2 13.3 %convert_reduce_fusion = (f32[3072]{0:T(1024)S(1)}, bf16[1024,3072]{1,0:T(8,128)(2,1)S(1)}) fusion(f32[1024,3072]{1,0:T(8,128)} %get-tuple-element.86, f32[3072]{0:T(1024)S(1)} %add.115, bf16[3072,768]{1,0:T(8,128)(2,1)S(1)} %bitcast.86, f32[1024,768]{1,0:T(8,128)S(1)} %get-tuple-element.58), kind=kOutput, calls=%fused_computation.6 | convolution fusion | flops 4879807488 | bytes 26763264 | tf_op jit(solution)/shard_map/td,fd->tf/dot_general | solution.py:901
  243.5 5.8 %multiply_reduce_fusion.1 = (f32[768]{0:T(1024)S(1)}, f32[1024]{0:T(1024)S(1)}, f32[1024]{0:T(1024)S(1)}, f32[768]{0:T(1024)S(1)}, f32[1024,768]{1,0:T(8,128)S(1)}) fusion(f32[1024,768]{1,0:T(8,128)S(1)} %copy-done.5, f32[1024]{0:T(1024)S(1)} %add_rsqrt_fusion.1, f32[1024]{0:T(1024)S(1)} %broadcast_multiply_fusion.4, f32[768]{0:T(1024)S(1)} %mul.152, ...), kind=kOutput, calls=%fused_computation.20 | convolution fusion | flops 4839698432 | bytes 20472832 | tf_op jit(solution)/shard_map/tf,df->td/dot_general | solution.py:905
  249.4 1.1 convert_reduce_fusion.3
  250.5 0.1 copy-done.19
  250.6 2.6 convolution_convert_fusion.3.g_ref
  253.2 27.2 %attend_grad.1 = bf16[1024,2304]{1,0:T(8,128)(2,1)} custom-call(bf16[1024,2304]{1,0:T(8,128)(2,1)} %add_convert_fusion.q_ref.k_ref.v_ref, bf16[1024,2304]{1,0:T(8,128)(2,1)} %add_convert_fusion.q_ref.k_ref.v_ref, bf16[1024,2304]{1,0:T(8,128)(2,1)} %add_convert_fusion.q_ref.k_ref.v_ref, bf16[1024,768]{1,0:T(8,128)(2,1)} %convolution_convert_fusion.3.g_ref, ...), custom_call_target="tpu_custom_call" | custom-call | tf_op jit(solution)/shard_map/attend_grad/pallas_call | solution.py:818
  280.4 8.6 %add_convert_fusion.1 = bf16[1024,768]{1,0:T(8,128)(2,1)} fusion(f32[1024,768]{1,0:T(8,128)S(1)} %get-tuple-element.60, bf16[1024,2304]{1,0:T(8,128)(2,1)} %attend_grad.1, bf16[768,2304]{1,0:T(8,128)(2,1)} %bitcast.88), kind=kOutput, calls=%fused_computation.16 | convolution fusion | flops 3625451520 | bytes 12976128 | tf_op jit(solution)/shard_map/te,de->td/dot_general | solution.py:916
  289.1 0.7 convert_reduce_fusion.1
  289.8 0.1 reshape.228
  289.9 0.1 reshape.229
  290.0 0.1 reshape.230
  290.0 0.1 reshape.231
  290.1 0.1 reshape.232
  290.2 0.1 reshape.236
  290.3 0.1 reshape.233
  290.4 0.1 reshape.234
  290.5 0.1 reshape.235
  290.5 0.1 concatenate.15
  290.7 0.7 copy.40
  291.4 9.8 %convolution_convert_fusion = bf16[3072,768]{1,0:T(8,128)(2,1)} fusion(bf16[1024,3072]{1,0:T(8,128)(2,1)} %get-tuple-element.85, f32[1024,768]{1,0:T(8,128)} %copy-done.7), kind=kOutput, calls=%fused_computation.12 | convolution fusion | flops 4834983936 | bytes 14155776 | tf_op jit(solution)/shard_map/tf,td->fd/dot_general | solution.py:900
  301.2 10.0 %convolution_convert_fusion.1 = bf16[768,3072]{1,0:T(8,128)(2,1)} fusion(bf16[1024,3072]{1,0:T(8,128)(2,1)} %copy-done.20, f32[1024,768]{1,0:T(8,128)S(1)} %copy-done.6, f32[768]{0:T(1024)S(1)} %add.112, f32[768]{0:T(1024)S(1)} %mul.152, f32[1024]{0:T(1024)S(1)} %add_rsqrt_fusion.1, f32[1024]{0:T(1024)S(1)} %broadcast_multiply_fusion.4), kind=kOutput, calls=%fused_computation.13 | convolution fusion | flops 4838129664 | bytes 14170112 | tf_op jit(solution)/shard_map/td,tf->df/dot_general | solution.py:904
  311.2 2.5 convolution_convert_fusion.4
  313.8 5.4 %convolution_convert_fusion.2 = bf16[768,2304]{1,0:T(8,128)(2,1)} fusion(bf16[1024,768]{1,0:T(8,128)(2,1)S(1)} %bitcast.91, bf16[1024,2304]{1,0:T(8,128)(2,1)S(1)} %bitcast.61), kind=kOutput, calls=%fused_computation.14 | convolution fusion | flops 3625648128 | bytes 9830400 | tf_op jit(solution)/shard_map/td,te->de/dot_general | solution.py:914
  319.1 138.0 %reduce_all.1 = (f32[24,2304]{1,0:T(8,128)}, f32[24,768]{1,0:T(8,128)}, f32[24,3072]{1,0:T(8,128)}, f32[96,768]{1,0:T(8,128)}, f32[8,128]{1,0:T(8,128)}, /*index...) custom-call(bf16[2,2,4,2,24,2304]{5,4,3,2,1,0:T(8,128)(2,1)} %bitcast.65, bf16[2,2,4,2,24,768]{5,4,3,2,1,0:T(8,128)(2,1)} %bitcast.67, ...), custom_call_target="tpu_custom_call" | custom-call | tf_op jit(solution)/shard_map/reduce_all/pallas_call | solution.py:685
  457.3 3.5 convert_element_type.124
  460.8 0.7 fusion.17
  461.4 0.6 fusion.20
  462.1 0.6 slice.109
  462.6 1.1 copy.47
  463.8 0.6 copy.48
  464.4 0.7 copy.49
  465.1 0.7 copy.50
  (68 shorter events, 0.3 us)
Async XLA Ops:
  0.7 170.2 %copy-start = (s32[8,4]{0,1:T(4,128)S(1)}, s32[8,4]{0,1:T(4,128)}, u32[]{:S(2)}) copy-start(s32[8,4]{0,1:T(4,128)} %param.20) | copy-start | bytes 388
  171.3 1.0 copy-start.15
  198.7 13.4 %copy-start.4 = (f32[1024,768]{1,0:T(8,128)}, f32[1024,768]{1,0:T(8,128)S(1)}, u32[]{:S(2)}) copy-start(f32[1024,768]{1,0:T(8,128)S(1)} %get-tuple-element.84) | copy-start | bytes 9437188
  223.5 4.6 copy-start.3
  223.5 6.7 %slice-start.4 = ((s8[4718592]{0:T(1024)(128)(4,1)}), s8[4194304]{0:T(1024)(128)(4,1)S(1)}, s32[]{:S(2)}) async-start(s8[4718592]{0:T(1024)(128)(4,1)} %bitcast.84), calls=%async_computation.4 | async-start | bytes 8388608
  228.1 2.1 slice-start.5
  228.8 14.7 %slice-start.2 = ((s8[4718592]{0:T(1024)(128)(4,1)}), s8[4194304]{0:T(1024)(128)(4,1)S(1)}, s32[]{:S(2)}) async-start(s8[4718592]{0:T(1024)(128)(4,1)} %bitcast.80), calls=%async_computation.2 | async-start | bytes 8388608
  230.1 13.3 %copy-start.7 = (f32[1024,768]{1,0:T(8,128)}, f32[1024,768]{1,0:T(8,128)S(1)}, u32[]{:S(2)}) copy-start(f32[1024,768]{1,0:T(8,128)S(1)} %get-tuple-element.58) | copy-start | bytes 9437188
  230.2 13.3 %copy-start.5 = (f32[1024,768]{1,0:T(8,128)S(1)}, f32[1024,768]{1,0:T(8,128)}, u32[]{:S(2)}) copy-start(f32[1024,768]{1,0:T(8,128)} %copy-done.4) | copy-start | bytes 9437188
  230.2 13.3 %slice-start.3 = ((s8[4718592]{0:T(1024)(128)(4,1)}), s8[524288]{0:T(1024)(128)(4,1)S(1)}, s32[]{:S(2)}) async-start(s8[4718592]{0:T(1024)(128)(4,1)} %bitcast.80), calls=%async_computation.3 | async-start | bytes 1048576
  243.5 5.9 %copy-start.20 = (bf16[1024,3072]{1,0:T(8,128)(2,1)}, bf16[1024,3072]{1,0:T(8,128)(2,1)S(1)}, u32[]{:S(2)}) copy-start(bf16[1024,3072]{1,0:T(8,128)(2,1)S(1)} %get-tuple-element.91) | copy-start | bytes 18874372
  249.4 1.3 copy-start.19
  250.5 29.9 %copy-start.8 = (f32[1024,768]{1,0:T(8,128)}, f32[1024,768]{1,0:T(8,128)S(1)}, u32[]{:S(2)}) copy-start(f32[1024,768]{1,0:T(8,128)S(1)} %get-tuple-element.60) | copy-start | bytes 9437188
  280.4 8.6 %copy-start.2 = (bf16[1024,2304]{1,0:T(8,128)(2,1)S(1)}, bf16[1024,2304]{1,0:T(8,128)(2,1)}, u32[]{:S(2)}) copy-start(bf16[1024,2304]{1,0:T(8,128)(2,1)} %attend_grad.1) | copy-start | bytes 14155780
  289.1 24.7 %slice-start = ((s8[4718592]{0:T(1024)(128)(4,1)}), s8[524288]{0:T(1024)(128)(4,1)S(1)}, s32[]{:S(2)}) async-start(s8[4718592]{0:T(1024)(128)(4,1)} %bitcast.60), calls=%async_computation | async-start | bytes 1048576
  291.3 9.8 %copy-start.6 = (f32[1024,768]{1,0:T(8,128)S(1)}, f32[1024,768]{1,0:T(8,128)}, u32[]{:S(2)}) copy-start(f32[1024,768]{1,0:T(8,128)} %copy-done.4) | copy-start | bytes 9437188
  291.4 22.4 %slice-start.1 = ((s8[4718592]{0:T(1024)(128)(4,1)}), s8[4194304]{0:T(1024)(128)(4,1)S(1)}, s32[]{:S(2)}) async-start(s8[4718592]{0:T(1024)(128)(4,1)} %bitcast.60), calls=%async_computation.1 | async-start | bytes 8388608
  301.2 10.1 %copy-start.9 = (f32[1024,768]{1,0:T(8,128)S(1)}, f32[1024,768]{1,0:T(8,128)}, u32[]{:S(2)}) copy-start(f32[1024,768]{1,0:T(8,128)} %copy-done.8) | copy-start | bytes 9437188
  301.2 10.1 %copy-start.18 = (bf16[1024,768]{1,0:T(8,128)(2,1)S(1)}, bf16[1024,768]{1,0:T(8,128)(2,1)}, u32[]{:S(2)}) copy-start(bf16[1024,768]{1,0:T(8,128)(2,1)} %get-tuple-element.36) | copy-start | bytes 4718596
  311.2 2.5 copy-start.17
  457.2 3.6 copy-start.13
  457.2 4.2 copy-start.16
  457.2 5.4 %copy-start.10 = (bf16[8,128,768]{2,1,0:T(8,128)(2,1)S(1)}, bf16[8,128,768]{2,1,0:T(8,128)(2,1)}, u32[]{:S(2)}) copy-start(bf16[8,128,768]{2,1,0:T(8,128)(2,1)} %get-tuple-element.111) | copy-start | bytes 4718596
  457.2 6.6 %copy-start.14 = (f32[24,768]{1,0:T(8,128)S(1)}, f32[24,768]{1,0:T(8,128)}, u32[]{:S(2)}) copy-start(f32[24,768]{1,0:T(8,128)} %get-tuple-element.118) | copy-start | bytes 221188
  457.2 7.2 %copy-start.12 = (f32[24,3072]{1,0:T(8,128)S(1)}, f32[24,3072]{1,0:T(8,128)}, u32[]{:S(2)}) copy-start(f32[24,3072]{1,0:T(8,128)} %get-tuple-element.122) | copy-start | bytes 884740
  457.2 8.6 %copy-start.1 = (s32[8,4]{0,1:T(4,128)S(1)}, s32[8,4]{0,1:T(4,128)}, u32[]{:S(2)}) copy-start(s32[8,4]{0,1:T(4,128)} %param.20) | copy-start | bytes 388
  460.8 4.4 copy-start.11
